TPU v7x, 128 devices: a whole 4x4x4 slice. The times are simulated.
128 devices in a mesh: rep: 2 (over core), dp: 64 (over x, y, z).
Axes of the slice: x: 4, y: 4, z: 4, core: 2. Of those that a mesh axis runs over, the one named last changes fastest.
Arguments:
- g_w_gate: bfloat16 [128, 2, 640, 3200], P(('rep', 'dp')), parts along dimension 0
- g_w_up: bfloat16 [128, 2, 640, 3200], P(('rep', 'dp')), parts along dimension 0
- g_w_down: bfloat16 [128, 2, 3200, 640], P(('rep', 'dp')), parts along dimension 0
- w_gate: bfloat16 [2, 640, 3200], replicated
- w_up: bfloat16 [2, 640, 3200], replicated
- w_down: bfloat16 [2, 3200, 640], replicated
- m_w_gate: float32 [2, 640, 3200], P(None, 'dp')
- m_w_up: float32 [2, 640, 3200], P(None, 'dp')
- m_w_down: float32 [2, 3200, 640], P(None, 'dp')
- v_w_gate: float32 [2, 640, 3200], P(None, 'dp')
- v_w_up: float32 [2, 640, 3200], P(None, 'dp')
- v_w_down: float32 [2, 3200, 640], P(None, 'dp')
Outputs:
- output 1: bfloat16 [4, 640, 3200], P('rep'), parts along dimension 0
- output 2: bfloat16 [4, 640, 3200], P('rep'), parts along dimension 0
- output 3: bfloat16 [4, 3200, 640], P('rep'), parts along dimension 0
- output 4: float32 [4, 640, 3200], P('rep', 'dp'), parts along dimension 0
- output 5: float32 [4, 640, 3200], P('rep', 'dp'), parts along dimension 0
- output 6: float32 [4, 3200, 640], P('rep', 'dp'), parts along dimension 0
- output 7: float32 [4, 640, 3200], P('rep', 'dp'), parts along dimension 0
- output 8: float32 [4, 640, 3200], P('rep', 'dp'), parts along dimension 0
- output 9: float32 [4, 3200, 640], P('rep', 'dp'), parts along dimension 0
There are 2 independent parts. A program takes and returns all parts, laid end to end along the dimension named above; an argument that names none is the same for every part.
All inputs are finite; a program needn't handle non-finite values.
Results may differ from a plain program's by a relative error of at most 0.022.
Values are sent between devices in bfloat16 or wider.
A program may use at most 1.5 GiB of HBM per device.

v0:
```python
import jax
import jax.numpy as jnp
from jax import lax
from jax.sharding import PartitionSpec as P


def adamw(w, m, v, g):
    m = 0.9 * m + 0.1 * g
    v = 0.95 * v + 0.05 * g * g
    step = m * lax.rsqrt(v + 1e-8) + 0.1 * w
    return (w - 0.02 * step).astype(jnp.bfloat16), m, v


def solution(mesh):
    def step(*arrays):
        terms, weights, m, v = (arrays[i : i + 3] for i in (0, 3, 6, 9))
        gradients = [lax.psum_scatter(t[0], "dp", scatter_dimension=1, tiled=True).astype(jnp.float32) for t in terms]
        me = lax.axis_index("dp")
        own = [lax.dynamic_slice_in_dim(w, me * one.shape[1], one.shape[1], 1).astype(jnp.float32) for w, one in zip(weights, m, strict=True)]
        new = [adamw(w, m, v, g) for w, m, v, g in zip(own, m, v, gradients, strict=True)]
        whole = [lax.all_gather(one[0], "dp", axis=1, tiled=True) for one in new]
        return (*whole, *(one[1] for one in new), *(one[2] for one in new))

    all_of, cut = P(None, None, None), P(None, "dp", None)
    return jax.shard_map(
        step,
        mesh=mesh,
        in_specs=(P(("rep", "dp"), None, None, None),) * 3 + (all_of,) * 3 + (cut,) * 6,
        out_specs=(P("rep", None, None),) * 3 + (P("rep", "dp", None),) * 6,
        check_vma=False,
    )
```

profile of v0, /device:TPU:0, one launch (start us, length us, event | category | flops | bytes accessed | tf_op | source)
XLA Modules:
  0.0 608.0 jit_solution(17883615352102886425)
XLA Ops:
  7.2 0.0 all-reduce.6.cloned.1.call-start
  7.2 0.0 copy-start
  7.2 0.0 copy-start.1
  7.2 38.5 %copy.48 = bf16[1,2,3200,640]{3,1,2,0:T(2,128)(2,1)} copy(bf16[1,2,3200,640]{3,2,1,0:T(8,128)(2,1)} %param.14) | data formatting | bytes 16384000 | tf_op args[2]
  45.8 0.0 copy-done
  45.8 0.0 copy-done.1
  45.8 40.0 %copy_bitcast_fusion.1 = (bf16[2,640,3200]{2,0,1:T(2,128)(2,1)}, bf16[2,640,3200]{2,0,1:T(2,128)(2,1)}) fusion(bf16[1,2,640,3200]{3,2,1,0:T(8,128)(2,1)S(1)} %copy-done, bf16[1,2,640,3200]{3,2,1,0:T(8,128)(2,1)S(1)} %copy-done.1), kind=kLoop, calls=%fused_computation.1 | loop fusion | bytes 32768000 | tf_op jit(solution)/shard_map/squeeze | solution.py:17
  85.7 0.0 copy-start.8
  85.7 0.0 copy-start.2
  85.8 0.0 copy-start.3
  85.8 0.0 copy-start.4
  85.8 0.0 copy-start.5
  85.8 0.0 copy-start.6
  85.8 0.0 copy-start.7
  85.8 0.0 all-reduce.6.cloned.1.call-update
  85.8 0.0 all-gather.6.cloned.1.call-start
  85.9 0.5 copy-done.8
  86.4 0.6 dynamic-slice
  87.6 1.2 constant_dynamic-slice_fusion.1
  88.8 265.4 %all-reduce.6.cloned.1.call-done = (bf16[2,640,3200]{2,0,1:T(2,128)(2,1)}, bf16[2,640,3200]{2,0,1:T(2,128)(2,1)}, bf16[2,3200,640]{2,0,1:T(2,128)(2,1)}) async-done(((bf16[2,640,3200]{2,0,1:T(2,128)(2,1)}, bf16[2,640,3200]{2,0,1:T(2,128)(2,1)}, bf16[2,3200,640]{2,0,1:T(2,128)(2,1)}), (bf16[2,640,3200]{2,0,1:T(2,128)(2,1)}, bf16[2,640,3200]{2,0,1:T(2,128)(2,1)}, ...) | async-done | bytes 24576016
  354.2 0.0 copy-done.2
  354.2 0.0 copy-done.3
  354.2 2.4 fusion.13
  356.6 0.0 all-gather.6.cloned.1.call-update
  356.7 0.0 all-gather.4.cloned.1.call-start
  356.7 0.0 copy-done.4
  356.7 0.0 copy-done.5
  356.7 2.4 fusion.12
  359.1 0.0 all-gather.4.cloned.1.call-update
  359.1 0.0 all-gather.8.cloned.1.call-start
  359.8 1.0 constant_dynamic-slice_fusion
  360.8 0.0 copy-done.6
  360.8 0.0 copy-done.7
  360.8 2.4 fusion.14
  363.2 0.0 all-gather.8.cloned.1.call-update
  363.2 70.3 %all-gather.6.cloned.1.call-done = bf16[2,640,3200]{2,0,1:T(2,128)(2,1)} async-done(((bf16[2,10,3200]{2,0,1:T(2,128)(2,1)}), bf16[2,640,3200]{2,0,1:T(2,128)(2,1)}) %all-gather.6.cloned.1.call-update) | async-done | bytes 8192016 | tf_op jit(solution)/shard_map/all_gather | solution.py:21
  433.5 7.6 %copy.37 = bf16[2,640,3200]{2,1,0:T(8,128)(2,1)} copy(bf16[2,640,3200]{2,0,1:T(2,128)(2,1)} %all-gather.6.cloned.1.call-done) | data formatting | bytes 16384000
  441.1 72.9 %all-gather.4.cloned.1.call-done = bf16[2,640,3200]{2,0,1:T(2,128)(2,1)} async-done(((bf16[2,10,3200]{2,0,1:T(2,128)(2,1)}), bf16[2,640,3200]{2,0,1:T(2,128)(2,1)}) %all-gather.4.cloned.1.call-update) | async-done | bytes 8192016 | tf_op jit(solution)/shard_map/all_gather | solution.py:21
  514.0 7.6 %copy.36 = bf16[2,640,3200]{2,1,0:T(8,128)(2,1)} copy(bf16[2,640,3200]{2,0,1:T(2,128)(2,1)} %all-gather.4.cloned.1.call-done) | data formatting | bytes 16384000
  521.6 72.1 %all-gather.8.cloned.1.call-done = bf16[2,3200,640]{2,0,1:T(2,128)(2,1)} async-done(((bf16[2,50,640]{2,0,1:T(2,128)(2,1)}), bf16[2,3200,640]{2,0,1:T(2,128)(2,1)}) %all-gather.8.cloned.1.call-update) | async-done | bytes 8192016 | tf_op jit(solution)/shard_map/all_gather | solution.py:21
  593.7 7.7 %copy.38 = bf16[2,3200,640]{2,1,0:T(8,128)(2,1)} copy(bf16[2,3200,640]{2,0,1:T(2,128)(2,1)} %all-gather.8.cloned.1.call-done) | data formatting | bytes 16384000
Async XLA Ops:
  7.2 347.0 %all-reduce.6.cloned.1.call-start = ((), (), s32[]{:S(2)}) async-start(), calls=%async_computation.3 | async-start | bytes 49152000
  7.2 38.5 %copy-start = (bf16[1,2,640,3200]{3,2,1,0:T(8,128)(2,1)S(1)}, bf16[1,2,640,3200]{3,2,1,0:T(8,128)(2,1)}, u32[]{:S(2)}) copy-start(bf16[1,2,640,3200]{3,2,1,0:T(8,128)(2,1)} %param.13) | copy-start | bytes 24576004
  7.2 38.5 %copy-start.1 = (bf16[1,2,640,3200]{3,2,1,0:T(8,128)(2,1)S(1)}, bf16[1,2,640,3200]{3,2,1,0:T(8,128)(2,1)}, u32[]{:S(2)}) copy-start(bf16[1,2,640,3200]{3,2,1,0:T(8,128)(2,1)} %param.12) | copy-start | bytes 24576004
  85.7 0.7 copy-start.8
  85.7 268.5 %copy-start.2 = (f32[2,10,3200]{2,0,1:T(2,128)S(1)}, f32[2,10,3200]{2,0,1:T(2,128)}, u32[]{:S(2)}) copy-start(f32[2,10,3200]{2,0,1:T(2,128)} %param.22) | copy-start | bytes 768004
  85.8 268.5 %copy-start.3 = (f32[2,10,3200]{2,0,1:T(2,128)S(1)}, f32[2,10,3200]{2,0,1:T(2,128)}, u32[]{:S(2)}) copy-start(f32[2,10,3200]{2,0,1:T(2,128)} %param.19) | copy-start | bytes 768004
  85.8 270.9 %copy-start.4 = (f32[2,10,3200]{2,0,1:T(2,128)S(1)}, f32[2,10,3200]{2,0,1:T(2,128)}, u32[]{:S(2)}) copy-start(f32[2,10,3200]{2,0,1:T(2,128)} %param.21) | copy-start | bytes 768004
  85.8 270.9 %copy-start.5 = (f32[2,10,3200]{2,0,1:T(2,128)S(1)}, f32[2,10,3200]{2,0,1:T(2,128)}, u32[]{:S(2)}) copy-start(f32[2,10,3200]{2,0,1:T(2,128)} %param.18) | copy-start | bytes 768004
  85.8 275.0 %copy-start.6 = (f32[2,50,640]{2,0,1:T(2,128)S(1)}, f32[2,50,640]{2,0,1:T(2,128)}, u32[]{:S(2)}) copy-start(f32[2,50,640]{2,0,1:T(2,128)} %param.23) | copy-start | bytes 768004
  85.8 275.0 %copy-start.7 = (f32[2,50,640]{2,0,1:T(2,128)S(1)}, f32[2,50,640]{2,0,1:T(2,128)}, u32[]{:S(2)}) copy-start(f32[2,50,640]{2,0,1:T(2,128)} %param.20) | copy-start | bytes 768004
  85.8 347.7 %all-gather.6.cloned.1.call-start = ((), (), s32[]{:S(2)}) async-start(), calls=%async_computation.1 | async-start | bytes 8320000 | tf_op jit(solution)/shard_map/all_gather | solution.py:21
  356.7 157.3 %all-gather.4.cloned.1.call-start = ((), (), s32[]{:S(2)}) async-start(), calls=%async_computation | async-start | bytes 8320000 | tf_op jit(solution)/shard_map/all_gather | solution.py:21
  359.1 234.6 %all-gather.8.cloned.1.call-start = ((), (), s32[]{:S(2)}) async-start(), calls=%async_computation.2 | async-start | bytes 8320000 | tf_op jit(solution)/shard_map/all_gather | solution.py:21
Sparse Core Ops, SparseCore 0:
  86.0 268.2 all-reduce.5
  357.7 75.8 all-gather.5
  437.0 76.9 all-gather.3
  516.7 76.9 all-gather.7
where the time goes:
time: 609 us; the launch traced here: 608 us
  waiting for transfers between devices  481 us (79%)
  local copies, waits for them, and re-layouts  105 us (17%)
  between operations  15.2 us (2%)
  other arithmetic  7.17 us (1%)
    unnamed x5, waiting for transfers between devices  265 us
    all_gather x3, waiting for transfers between devices, step(): whole = [lax.all_gather(one[0], 'dp', axis=1, tiled=True) for one in new]  215 us
    unnamed x23, local copies, waits for them, and re-layouts  62.6 us
    squeeze x1, local copies, waits for them, and re-layouts, step(): t[0]  40 us
  transfers between devices with their start and end apart: 4, of which 4 were waited for; matrix products, arithmetic and copies ran while one was open for 4% of the time, Pallas kernels for 0%

commit v1 on v0

v1 whole, which is shorter than its diff:
```python
import functools
import heapq

import jax
import jax.numpy as jnp
from jax import lax
from jax.experimental import pallas as pl
from jax.experimental.pallas import tpu as pltpu
from jax.sharding import PartitionSpec as P

BF16, F32 = jnp.bfloat16, jnp.float32
MESH = pl.DeviceIdType.MESH
SIGN = (1, -1)
ORDER = (((0, 1, 2), (0, 1, 2)), ((1, 0, 2), (1, 0, 2)), ((2, 0, 1), (2, 1, 0)))
FLOWS = tuple((w, l) for w in range(3) for l in range(2))


def adamw(w, m, v, g):
    m = 0.9 * m + 0.1 * g
    v = 0.95 * v + 0.05 * g * g
    step = m * lax.rsqrt(v + 1e-8) + 0.1 * w
    return (w - 0.02 * step).astype(BF16), m, v


def in_order(first, tasks, sends):
    rate, trip = 46.6e3, 2.2
    free, arrived, done, order = {}, {}, {}, []

    def send(message, at):
        link, size = sends[message]
        start = max(free.get(link, 0.0), at)
        free[link] = start + size / rate
        arrived[message] = free[link] + trip

    for message in first:
        send(message, 0.0)
    now, left = 0.0, dict(tasks)
    while left:
        ready = []
        for place, (task, (message, before, _, _)) in enumerate(left.items()):
            if message in arrived and all(b in done for b in before):
                ready.append((max([arrived[message]] + [done[b] for b in before]), place, task))
        at, _, task = min(ready)
        now = max(now, at) + left[task][2]
        done[task] = now
        for message in left.pop(task)[3]:
            send(message, now)
        order.append(task)
    return order


def place():
    me = lax.axis_index("dp")
    return lax.div(me, 16), lax.rem(lax.div(me, 4), 4), lax.rem(me, 4)


def towards(at, axis, sign):
    to = list(at)
    to[axis] = lax.rem(at[axis] + 4 + sign, 4)
    return {"dp": to[0] * 16 + to[1] * 4 + to[2]}


def ring(p, sign, steps):
    return lax.rem(p + 8 - sign * steps, 4)


def meet(at):
    barrier = pltpu.get_barrier_semaphore()
    for axis in range(3):
        for sign in SIGN:
            pl.semaphore_signal(barrier, inc=1, device_id=towards(at, axis, sign), device_id_type=MESH)
    pl.semaphore_wait(barrier, 6)


def rows8(i, size):
    return pl.ds(pl.multiple_of(i, 8), size)


def pieces(ref, body):
    if len(ref.shape) == 3:
        steps, index = ref.shape[0], lambda j: (j,)
    elif ref.shape[1] == 3200:
        steps, index = 5, lambda j: (slice(None), pl.ds(pl.multiple_of(j * 640, 128), 640))
    else:
        return body((slice(None), slice(None)))
    lax.fori_loop(0, steps, lambda j, _: (body(index(j)), 0)[1], 0)


def add_to(out, a, b):
    def one(i):
        out[i] = (a[i].astype(F32) + b[i].astype(F32)).astype(BF16)

    pieces(out, one)


CELL = (40 * 3200 * 2, 40 * 3200 * 2, 4 * 56 * 640 * 2)
LAST = (16 * 3200 * 2, 16 * 3200 * 2, 56 * 640 * 2)


def sum_order():
    tasks, sends, first = {}, {}, []
    for t in range(3):
        for k in range(4):
            for w, l in FLOWS:
                a, b, c = ORDER[w][l]
                m = ("a", w, l, t, k)
                sends[m] = ((a, l), CELL[w])
                if t == 0:
                    first.append(m)
                nxt = [("a", w, l, t + 1, k)] if t < 2 else [("b", w, l, 0)] if k == 0 else []
                tasks[m] = (m, [], CELL[w] / 2 / 1024 * 5 / 1900, nxt)
    for w, l in FLOWS:
        a, b, c = ORDER[w][l]
        for t in range(3):
            m = ("b", w, l, t)
            sends[m] = ((b, l), CELL[w])
            tasks[m] = (m, [("a", w, l, 2, t + 1)], CELL[w] / 2 / 1024 * 5 / 1900, [("b", w, l, t + 1)] if t < 2 else [("c", w, l, 0)])
            m = ("c", w, l, t)
            sends[m] = ((c, l), LAST[w])
            tasks[m] = (m, [("b", w, l, 2)], LAST[w] / 2 / 1024 * 5 / 1900, [("c", w, l, t + 1)] if t < 2 else [])
    return in_order(first, tasks, sends)


def sum_kernel(*refs):
    terms, outs = refs[:3], refs[3:6]
    r1, mine, r2, r3 = refs[6:9], refs[9:12], refs[12:15], refs[15:18]
    load_sem, a_send, a_recv, b_send, b_recv, c_send, c_recv = refs[18:]
    at = place()

    def source(w, l, block, k):
        a, b, _ = ORDER[w][l]
        chunk = ring(at[b], SIGN[l], 1 + k)
        if w < 2:
            i, j = (block, chunk) if a == 0 else (chunk, block)
            return terms[w].at[l, i, j]
        window = rows8(block * 48, 56)
        return terms[w].at[l, chunk, :, window, :] if b == 0 else terms[w].at[l, :, chunk, window, :]

    def load(w, l, t, k):
        block = ring(at[ORDER[w][l][0]], SIGN[l], 2 + t)
        return pltpu.make_async_copy(source(w, l, block, k), mine[w].at[l, t, k], load_sem.at[w, l, t, k])

    def last(w, l, t):
        block = ring(at[ORDER[w][l][2]], SIGN[l], 2 + t)
        return r2[w].at[l, 2, rows8(block * 8, 16), :] if w < 2 else r2[w].at[l, 2, block]

    def message(name, w, l, t, k=0):
        a, b, c = ORDER[w][l]
        if name == "a":
            src = source(w, l, ring(at[a], SIGN[l], 1), k) if t == 0 else r1[w].at[l, t - 1, k]
            dst, sems, axis = r1[w].at[l, t, k], (a_send.at[w, l, t, k], a_recv.at[w, l, t, k]), a
        elif name == "b":
            src = r1[w].at[l, 2, 0] if t == 0 else r2[w].at[l, t - 1]
            dst, sems, axis = r2[w].at[l, t], (b_send.at[w, l, t], b_recv.at[w, l, t]), b
        else:
            src = last(w, l, -1) if t == 0 else r3[w].at[l, t - 1]
            dst, sems, axis = r3[w].at[l, t], (c_send.at[w, l, t], c_recv.at[w, l, t]), c
        return pltpu.make_async_remote_copy(
            src_ref=src, dst_ref=dst, send_sem=sems[0], recv_sem=sems[1], device_id=towards(at, axis, SIGN[l]), device_id_type=MESH
        )

    order = sum_order()
    for name, *key in order:
        if name == "a":
            load(*key).start()
    meet(at)
    for k in range(4):
        for w, l in FLOWS:
            message("a", w, l, 0, k).start()
    for name, w, l, t, *k in order:
        message(name, w, l, t, *k).wait_recv()
        if name == "a":
            load(w, l, t, *k).wait()
            to = r1[w].at[l, t, k[0]]
            add_to(to, to, mine[w].at[l, t, k[0]])
            if t < 2:
                message("a", w, l, t + 1, *k).start()
            elif k[0] == 0:
                message("b", w, l, 0).start()
        elif name == "b":
            to = r2[w].at[l, t]
            add_to(to, to, r1[w].at[l, 2, t + 1])
            message(*(("b", w, l, t + 1) if t < 2 else ("c", w, l, 0))).start()
        else:
            to = r3[w].at[l, t] if t < 2 else outs[w].at[l]
            add_to(to, r3[w].at[l, t], last(w, l, t))
            if t < 2:
                message("c", w, l, t + 1).start()
    for name, *key in order:
        message(name, *key).wait_send()


def summed(terms):
    cells = ((40, 3200), (40, 3200), (4, 56, 640))
    ends = ((16, 3200), (16, 3200), (56, 640))
    dma = pltpu.SemaphoreType.DMA
    return pl.pallas_call(
        sum_kernel,
        out_shape=[jax.ShapeDtypeStruct((2, *e), BF16) for e in ends],
        in_specs=[pl.BlockSpec(memory_space=pltpu.HBM)] * 3,
        out_specs=[pl.BlockSpec(memory_space=pltpu.VMEM)] * 3,
        scratch_shapes=[
            *(pltpu.VMEM((2, 3, 4, *c), BF16) for c in cells),
            *(pltpu.VMEM((2, 3, 4, *c), BF16) for c in cells),
            *(pltpu.VMEM((2, 3, *c), BF16) for c in cells),
            *(pltpu.VMEM((2, 3, *e), BF16) for e in ends),
            dma((3, 2, 3, 4)),
            *(dma((3, 2, 3, 4)),) * 2,
            *(dma((3, 2, 3)),) * 4,
        ],
        compiler_params=pltpu.CompilerParams(collective_id=0, has_side_effects=True, vmem_limit_bytes=60 * 2**20),
        name="sum_terms",
    )(*terms)


def gather_order():
    tasks, sends, first = {}, {}, []
    for w, l in FLOWS:
        c, b, a = ORDER[w][l]
        first.append(("a", w, l, 0))
        for t in range(3):
            m = ("a", w, l, t)
            sends[m] = ((a, l), LAST[w])
            nxt = [("a", w, l, t + 1)] if t < 2 else [("b", w, l, 0), ("c", w, l, 0, 0)]
            tasks[m] = (m, [], 0.05 + (0.5 if t == 2 and w < 2 else 0), nxt)
            m = ("b", w, l, t)
            sends[m] = ((b, l), CELL[w])
            tasks[m] = (m, [("a", w, l, 2)], 0.05, ([("b", w, l, t + 1)] if t < 2 else []) + [("c", w, l, 0, t + 1)])
    for t in range(3):
        for k in range(4):
            for w, l in FLOWS:
                c, b, a = ORDER[w][l]
                m = ("c", w, l, t, k)
                sends[m] = ((c, l), CELL[w])
                tasks[m] = (m, [("b", w, l, 2)], 0.05, [("c", w, l, t + 1, k)] if t < 2 else [])
    return in_order(first, tasks, sends)


def gather_kernel(*refs):
    new, outs = refs[:3], refs[3:6]
    ends, cell, down = refs[6:8], refs[8:10], refs[10]
    own_sem, put_sem, a_send, a_recv, b_send, b_recv, c_send, c_recv = refs[11:]
    at = place()
    x, y, z = at

    def message(name, w, l, t, k=0):
        c, b, a = ORDER[w][l]
        s = SIGN[l]
        if name == "a":
            block = ring(at[a], s, t)
            if w < 2:
                dst = ends[w].at[l, block]
            else:
                dst = down.at[l, z, x, block] if a == 1 else down.at[l, z, block, y]
            src = new[w].at[l] if t == 0 else dst
            sems, axis = (a_send.at[w, l, t], a_recv.at[w, l, t]), a
        elif name == "b":
            block = ring(at[b], s, t)
            if w < 2:
                dst = outs[w].at[l, x, block] if b == 1 else outs[w].at[l, block, y]
                src = cell[w].at[l] if t == 0 else dst
            else:
                dst = src = down.at[l, z, :, block] if b == 1 else down.at[l, z, block]
            sems, axis = (b_send.at[w, l, t], b_recv.at[w, l, t]), b
        else:
            block, chunk = ring(at[c], s, t), ring(at[b], s, k)
            if w < 2:
                dst = outs[w].at[l, block, chunk] if c == 0 else outs[w].at[l, chunk, block]
                src = cell[w].at[l] if t == k == 0 else dst
            else:
                dst = src = down.at[l, block, :, chunk] if b == 1 else down.at[l, block, chunk]
            sems, axis = (c_send.at[w, l, t, k], c_recv.at[w, l, t, k]), c
        return pltpu.make_async_remote_copy(
            src_ref=src, dst_ref=dst, send_sem=sems[0], recv_sem=sems[1], device_id=towards(at, axis, s), device_id_type=MESH
        )

    def own(w, l):
        if w < 2:
            return pltpu.make_async_copy(cell[w].at[l], outs[w].at[l, x, y], own_sem.at[w, l])
        return None

    def keep(w, l):
        to = ends[w].at[l, z] if w < 2 else down.at[l, z, x, y]

        def one(i):
            to[i] = new[w].at[l][i]

        pieces(to, one)

    def join(w, l):
        def one(j, _):
            cols = pl.ds(pl.multiple_of(j * 640, 128), 640)
            row = lax.broadcasted_iota(jnp.int32, (8, 640), 0)
            top = [ends[w][l, i, 0:8, cols].astype(F32) for i in range(4)]
            low = [ends[w][l, i, 8:16, cols].astype(F32) for i in range(4)]
            tiles = [top[0], *(jnp.where(row < 2 * i, low[i - 1], top[i]) for i in (1, 2, 3)), low[3]]
            for i, tile in enumerate(tiles):
                cell[w][l, 8 * i : 8 * i + 8, cols] = tile.astype(BF16)
            return 0

        lax.fori_loop(0, 5, one, 0)

    def part(l, i, j, q):
        first = 0 if q == 0 else 8
        return down.at[l, q, i, j, first:56, :], outs[2].at[l, i, j, 48 * q + first : 48 * q + 56, :]

    def mend(l, k):
        b = ORDER[2][l][1]
        chunk = ring(at[b], SIGN[l], k)

        def one(n, _):
            i, j = (n, chunk) if b == 1 else (chunk, n)
            row = lax.broadcasted_iota(jnp.int32, (8, 640), 0)
            for q in range(3):
                low = down[l, q, i, j, 48:56, :].astype(F32)
                top = down[l, q + 1, i, j, 0:8, :].astype(F32)
                down[l, q, i, j, 48:56, :] = jnp.where(row < 2 * q + 2, low, top).astype(BF16)
            return 0

        lax.fori_loop(0, 4, one, 0)

    def put(l, k):
        b = ORDER[2][l][1]
        chunk = ring(at[b], SIGN[l], k)
        i, j = (slice(None), chunk) if b == 1 else (chunk, slice(None))
        return [pltpu.make_async_copy(*part(l, i, j, q), put_sem.at[l, k, q]) for q in range(4)]

    order, waited = gather_order(), set()
    meet(at)
    for w, l in FLOWS:
        message("a", w, l, 0).start()
    for w, l in FLOWS:
        keep(w, l)
    for name, w, l, t, *k in order:
        message(name, w, l, t, *k).wait_recv()
        if name == "a":
            if t < 2:
                message("a", w, l, t + 1).start()
            else:
                if w < 2:
                    join(w, l)
                message("b", w, l, 0).start()
                message("c", w, l, 0, 0).start()
                if w < 2:
                    own(w, l).start()
        elif name == "b":
            if t < 2:
                message("b", w, l, t + 1).start()
            message("c", w, l, 0, t + 1).start()
        elif t < 2:
            message("c", w, l, t + 1, *k).start()
        elif w == 2:
            over = [("c", w, l, step, *k) for step in range(3)]
            over += [("b", w, l, *k)] if k[0] < 3 else []
            over += [("a", w, l, step) for step in range(3)] if k[0] == 0 else []
            for sent in over:
                message(*sent).wait_send()
            waited.update(over)
            mend(l, *k)
            for copy in put(l, *k):
                copy.start()
    for task in order:
        if task not in waited:
            message(*task).wait_send()
    for w, l in FLOWS:
        if w < 2:
            own(w, l).wait()
    for l in range(2):
        for k in range(4):
            for copy in put(l, k):
                copy.wait()


def gathered(new):
    dma = pltpu.SemaphoreType.DMA
    shapes = ((2, 4, 4, 40, 3200),) * 2 + ((2, 4, 4, 200, 640),)
    return pl.pallas_call(
        gather_kernel,
        out_shape=[jax.ShapeDtypeStruct(s, BF16) for s in shapes],
        in_specs=[pl.BlockSpec(memory_space=pltpu.VMEM)] * 3,
        out_specs=[pl.BlockSpec(memory_space=pl.ANY)] * 3,
        scratch_shapes=[
            *(pltpu.VMEM((2, 4, 16, 3200), BF16),) * 2,
            *(pltpu.VMEM((2, 40, 3200), BF16),) * 2,
            pltpu.VMEM((2, 4, 4, 4, 56, 640), BF16),
            dma((2, 2)),
            dma((2, 4, 4)),
            *(dma((3, 2, 3)),) * 4,
            *(dma((3, 2, 3, 4)),) * 2,
        ],
        compiler_params=pltpu.CompilerParams(collective_id=1, has_side_effects=True, vmem_limit_bytes=20 * 2**20),
        name="gather_weights",
    )(*new)


def solution(mesh):
    def step(*arrays):
        terms, weights, m, v = (arrays[i : i + 3] for i in (0, 3, 6, 9))
        me = lax.axis_index("dp")
        z = lax.rem(me, 4)
        windows = summed([t.reshape(s) for t, s in zip(terms, ((2, 4, 4, 40, 3200),) * 2 + ((2, 4, 4, 200, 640),), strict=True)])
        gradients = [lax.dynamic_slice_in_dim(g, 2 * z, one.shape[1], 1).astype(F32) for g, one in zip(windows, m, strict=True)]
        own = [lax.dynamic_slice_in_dim(w, me * one.shape[1], one.shape[1], 1).astype(F32) for w, one in zip(weights, m, strict=True)]
        new = [adamw(w, m, v, g) for w, m, v, g in zip(own, m, v, gradients, strict=True)]
        put = [lax.dynamic_update_slice_in_dim(jnp.zeros_like(g), one[0], 2 * z, 1) for g, one in zip(windows, new, strict=True)]
        whole = [o.reshape(w.shape) for o, w in zip(gathered(put), weights, strict=True)]
        return (*whole, *(one[1] for one in new), *(one[2] for one in new))

    all_of, cut = P(None, None, None), P(None, "dp", None)
    return jax.shard_map(
        step,
        mesh=mesh,
        in_specs=(P(("rep", "dp"), None, None, None),) * 3 + (all_of,) * 3 + (cut,) * 6,
        out_specs=(P("rep", None, None),) * 3 + (P("rep", "dp", None),) * 6,
        check_vma=False,
    )
```

time: 609 us -> 288 us (0.47)
  waiting for transfers between devices: 481 us -> 0 us
  Pallas kernels: 0 us -> 249 us
  local copies, waits for them, and re-layouts: 105 us -> 35.2 us
  between operations: 15.2 us -> 0.84 us
    unnamed x5 -> x0, waiting for transfers between devices: 265 us -> none
    pallas_call x0 -> x2, Pallas kernels: none -> 249 us  [the longest x1 125 us: summed(): pl.pallas_call(sum_kernel, out_shape=[jax.ShapeDtypeStruct((2, *e), BF16)...]
    all_gather x3 -> x0, waiting for transfers between devices: 215 us -> none  [step(): whole = [lax.all_gather(one[0], 'dp', axis=1, tiled=True) for one in new]]
    squeeze x1 -> x0, local copies, waits for them, and re-layouts: 40 us -> none  [step(): t[0]]
    unnamed x23 -> x37, local copies, waits for them, and re-layouts: 62.6 us -> 32.7 us
  transfers between devices with their start and end apart: 4 -> 0, of which waited for: 4 -> 0; matrix products, arithmetic and copies ran while one was open for 4% -> 0% of each run, Pallas kernels for 0% -> 0%
where the time goes in v1:
time: 288 us
  Pallas kernels  249 us (86%)
  local copies, waits for them, and re-layouts  35.2 us (12%)
  other arithmetic  3.06 us (1%)
    pallas_call x1, Pallas kernels, summed(): pl.pallas_call(sum_kernel, out_shape=[jax.ShapeDtypeStruct((2, *e), BF16)...  125 us
    pallas_call x1, Pallas kernels, gathered(): pl.pallas_call(gather_kernel, out_shape=[jax.ShapeDtypeStruct(s, BF16) fo...  124 us
    unnamed x37, local copies, waits for them, and re-layouts  32.7 us

profile of v1, /device:TPU:0, one launch (start us, length us, event | category | flops | bytes accessed | tf_op | source)
XLA Modules:
  0.0 288.1 jit_solution(156391874176617942)
XLA Ops:
  0.7 0.0 copy-start.12
  0.7 0.0 copy-start.13
  0.7 0.0 copy-start.8
  0.7 0.0 copy-start.9
  0.7 0.0 copy-start.10
  0.7 0.0 copy-start.11
  0.7 124.6 %sum_terms.1 = (bf16[2,16,3200]{2,1,0:T(8,128)(2,1)}, bf16[2,16,3200]{2,1,0:T(8,128)(2,1)}, bf16[2,56,640]{2,1,0:T(8,128)(2,1)}) custom-call(bf16[2,4,4,40,3200]{4,3,2,1,0:T(8,128)(2,1)} %bitcast.9, bf16[2,4,4,40,3200]{4,3,2,1,0:T(8,128)(2,1)} %bitcast.10, bf16[2,4,4,200,640]{4,3,2,1,0:T(8,128)(2,1)} %bitcast.11), custom_call_target="tpu_custom_call" | custom-call | tf_op jit(solution)/shard_map/sum_terms/pallas_call | solution.py:197
  125.3 0.0 copy-done.12
  125.3 0.0 copy-done.13
  125.3 1.2 fusion.12
  126.5 0.6 dynamic_update_slice.11.refs_2_
  127.2 0.0 copy-start.6
  127.2 0.8 copy.32
  128.0 0.8 copy.29
  128.8 0.0 copy-done.8
  128.8 0.0 copy-done.9
  128.9 0.0 copy-done.10
  128.9 0.0 copy-done.11
  128.9 1.9 fusion.2
  130.7 0.0 copy-done.6
  130.7 0.9 dynamic_update_slice.10.refs_1_
  131.7 0.0 copy-start.4
  131.7 0.7 copy-done.4
  132.4 0.9 dynamic_update_slice.9.refs_0_
  133.3 0.0 copy-start.2
  133.3 0.8 copy.30
  134.2 0.8 copy.27
  135.0 0.8 copy.31
  135.8 0.0 copy-done.2
  135.8 0.8 copy.28
  136.6 0.0 copy-start.3
  136.6 0.9 copy-done.3
  137.6 0.0 copy-start.5
  137.6 0.9 copy-done.5
  138.5 0.0 copy-start.7
  138.5 0.9 copy-done.7
  139.4 124.4 %gather_weights.1 = (bf16[2,4,4,40,3200]{4,3,2,1,0:T(8,128)(2,1)S(1)}, bf16[2,4,4,40,3200]{4,3,2,1,0:T(8,128)(2,1)S(1)}, bf16[2,4,4,200,640]{4,3,2,1,0:T(8,128)(2,1)S(1)}) custom-call(bf16[2,16,3200]{2,1,0:T(8,128)(2,1)S(1)} %copy-done.3, bf16[2,16,3200]{2,1,0:T(8,128)(2,1)S(1)} %copy-done.5, bf16[2,56,640]{2,1,0:T(8,128)(2,1)S(1)} %copy-done.7), custom_call_target="tpu_custom_call" | custom-call | tf_op jit(solution)/shard_map/gather_weights/pallas_call | solution.py:377
  263.9 0.0 copy-start
  263.9 3.2 %copy-done = bf16[2,4,4,40,3200]{4,3,2,1,0:T(8,128)(2,1)} copy-done((bf16[2,4,4,40,3200]{4,3,2,1,0:T(8,128)(2,1)}, bf16[2,4,4,40,3200]{4,3,2,1,0:T(8,128)(2,1)S(1)}, u32[]{:S(2)}) %copy-start) | copy-done | bytes 8192024
  267.0 0.0 copy-start.1
  267.0 3.3 %copy-done.1 = bf16[2,4,4,40,3200]{4,3,2,1,0:T(8,128)(2,1)} copy-done((bf16[2,4,4,40,3200]{4,3,2,1,0:T(8,128)(2,1)}, bf16[2,4,4,40,3200]{4,3,2,1,0:T(8,128)(2,1)S(1)}, u32[]{:S(2)}) %copy-start.1) | copy-done | bytes 8192024
  270.4 7.2 %copy.63 = bf16[2,640,3200]{2,1,0:T(8,128)(2,1)} copy(bf16[2,640,3200]{2,1,0:T(8,128)(2,1)} %bitcast.8) | data formatting | bytes 16384000
  277.6 7.2 %copy.64 = bf16[2,640,3200]{2,1,0:T(8,128)(2,1)} copy(bf16[2,640,3200]{2,1,0:T(8,128)(2,1)} %bitcast.7) | data formatting | bytes 16384000
  284.8 3.3 %copy.65 = bf16[2,3200,640]{2,1,0:T(8,128)(2,1)} copy(bf16[2,3200,640]{2,1,0:T(8,128)(2,1)S(1)} %bitcast.6) | data formatting | bytes 16384000
  (3 shorter events, 0.0 us)
Async XLA Ops:
  0.7 124.6 %copy-start.12 = (f32[2,50,640]{2,0,1:T(2,128)S(1)}, f32[2,50,640]{2,0,1:T(2,128)}, u32[]{:S(2)}) copy-start(f32[2,50,640]{2,0,1:T(2,128)} %param.23) | copy-start | bytes 768004
  0.7 124.6 %copy-start.13 = (f32[2,50,640]{2,0,1:T(2,128)S(1)}, f32[2,50,640]{2,0,1:T(2,128)}, u32[]{:S(2)}) copy-start(f32[2,50,640]{2,0,1:T(2,128)} %param.20) | copy-start | bytes 768004
  0.7 128.2 %copy-start.8 = (f32[2,10,3200]{2,0,1:T(2,128)S(1)}, f32[2,10,3200]{2,0,1:T(2,128)}, u32[]{:S(2)}) copy-start(f32[2,10,3200]{2,0,1:T(2,128)} %param.21) | copy-start | bytes 768004
  0.7 128.2 %copy-start.9 = (f32[2,10,3200]{2,0,1:T(2,128)S(1)}, f32[2,10,3200]{2,0,1:T(2,128)}, u32[]{:S(2)}) copy-start(f32[2,10,3200]{2,0,1:T(2,128)} %param.18) | copy-start | bytes 768004
  0.7 128.2 %copy-start.10 = (f32[2,10,3200]{2,0,1:T(2,128)S(1)}, f32[2,10,3200]{2,0,1:T(2,128)}, u32[]{:S(2)}) copy-start(f32[2,10,3200]{2,0,1:T(2,128)} %param.22) | copy-start | bytes 768004
  0.7 128.1 %copy-start.11 = (f32[2,10,3200]{2,0,1:T(2,128)S(1)}, f32[2,10,3200]{2,0,1:T(2,128)}, u32[]{:S(2)}) copy-start(f32[2,10,3200]{2,0,1:T(2,128)} %param.19) | copy-start | bytes 768004
  127.2 3.5 %copy-start.6 = (bf16[2,56,640]{2,1,0:T(8,128)(2,1)}, bf16[2,56,640]{2,1,0:T(8,128)(2,1)S(1)}, u32[]{:S(2)}) copy-start(bf16[2,56,640]{2,1,0:T(8,128)(2,1)S(1)} %dynamic_update_slice.11.refs_2_) | copy-start | bytes 430084
  131.7 0.7 copy-start.4
  133.3 2.5 copy-start.2
  136.6 0.9 copy-start.3
  137.6 0.9 copy-start.5
  138.5 0.9 copy-start.7
  263.9 3.2 %copy-start = (bf16[2,4,4,40,3200]{4,3,2,1,0:T(8,128)(2,1)}, bf16[2,4,4,40,3200]{4,3,2,1,0:T(8,128)(2,1)S(1)}, u32[]{:S(2)}) copy-start(bf16[2,4,4,40,3200]{4,3,2,1,0:T(8,128)(2,1)S(1)} %get-tuple-element.19) | copy-start | bytes 24576004
  267.0 3.3 %copy-start.1 = (bf16[2,4,4,40,3200]{4,3,2,1,0:T(8,128)(2,1)}, bf16[2,4,4,40,3200]{4,3,2,1,0:T(8,128)(2,1)S(1)}, u32[]{:S(2)}) copy-start(bf16[2,4,4,40,3200]{4,3,2,1,0:T(8,128)(2,1)S(1)} %get-tuple-element.18) | copy-start | bytes 24576004

commit v2 on v0

v2 whole, which is shorter than its diff:
```python
import jax
import jax.numpy as jnp
from jax import lax
from jax.experimental import pallas as pl
from jax.experimental.pallas import tpu as pltpu
from jax.sharding import PartitionSpec as P

BF16, F32 = jnp.bfloat16, jnp.float32
MESH = pl.DeviceIdType.MESH
SIGN = (1, -1)
COLS = (((0, 3200),),) * 2 + (((0, 640),),)
HALVES = (0,)
XYZ, YXZ, ZXY, ZYX = (0, 1, 2), (1, 0, 2), (2, 0, 1), (2, 1, 0)
ORDER = (((XYZ, XYZ),) * 2, ((YXZ, YXZ),) * 2, ((ZXY, ZYX), (ZYX, ZXY)))
FLOWS = tuple((w, l, h) for h in HALVES for w in range(3) for l in range(2))
CELL, OWNED, APART, WINDOW = (40, 40, 200), (10, 10, 50), (8, 8, 48), (16, 16, 56)
WIDTH = (3200, 3200, 640)


def plan():
    ahead, rate, trip = 1.0, 46.6e3, 2.2
    sizes, tasks = {}, {}
    for w, l, h in FLOWS:
        one, two, three = ((axis, l) for axis in ORDER[w][l][h])
        width = COLS[w][h][1] * 2
        whole, back, last = width * (40 if w < 2 else 224), width * (40 if w < 2 else 192), width * WINDOW[w]
        add = 5 / 2 / 1024 / 1900
        for t in range(3):
            on = t < 2
            for k in range(4):
                a = ("a", w, l, h, t, k)
                sizes[a] = (one, whole, 1 + h)
                then = [("a", w, l, h, t + 1, k)] if on else [("b", w, l, h, 0)] if k == 0 else []
                then += [("a", w, l, h + 1, 0, k)] if t == 1 and h + 1 < len(HALVES) else []
                tasks[a] = (a, [], whole * add, then)
                r = ("r", w, l, h, t, k)
                sizes[r] = (one, back, 5 + h)
                tasks[r] = (r, [("q", w, l, h, 2)], 0.05, [("r", w, l, h, t + 1, k)] if on else [])
            b, c, p, q = ((name, w, l, h, t) for name in "bcpq")
            sizes.update({b: (two, whole, 0), c: (three, last, 0), p: (three, last, 0), q: (two, back, 0)})
            tasks[b] = (b, [("a", w, l, h, 2, t + 1)], whole * add, [("b", w, l, h, t + 1)] if on else [("c", w, l, h, 0)])
            tasks[c] = (c, [("b", w, l, h, 2)], last * add, [("c", w, l, h, t + 1)] if on else [])
            tasks[p] = (p, [("step", w, h)], 0.05 if on else 0.4, [("p", w, l, h, t + 1)] if on else [("q", w, l, h, 0), ("r", w, l, h, 0, 0)])
            tasks[q] = (q, [("p", w, l, h, 2)], 0.05, ([("q", w, l, h, t + 1)] if on else []) + [("r", w, l, h, 0, t + 1)])
    for h in HALVES:
        for w in range(3):
            tasks["step", w, h] = (None, [("c", w, l, h, 2) for l in range(2)], 1.5, [("p" if w < 2 else "e", w, l, h, 0) for l in range(2)])
        for l in range(2):
            e = ("e", 2, l, h, 0)
            sizes[e] = ((2, 1), 16 * COLS[2][h][1], 0)
            tasks[e] = (e, [("step", 2, h)], 0.1, [("p", 2, l, h, 0)])
    waiting, free, arrived, done, steps, count = {}, {}, {}, {}, [], 0

    def push(message):
        nonlocal count
        link, _, rank = sizes[message]
        waiting.setdefault(link, []).append((rank, count, message))
        waiting[link].sort()
        count += 1

    for k in range(4):
        for w in range(3):
            for l in range(2):
                push(("a", w, l, 0, 0, k))
    now = 0.0
    while tasks:
        issued = True
        while issued:
            ready = []
            for place, (task, (message, before, _, _)) in enumerate(tasks.items()):
                if (message is None or message in arrived) and all(b in done for b in before):
                    ready.append((max([arrived.get(message, 0.0)] + [done[b] for b in before]), place, task))
            at, _, task = min(ready) if ready else (now, 0, None)
            until, issued = max(now + ahead, at + 1.0), False
            for link in sorted(waiting):
                while waiting[link] and free.get(link, 0.0) < until:
                    message = waiting[link].pop(0)[2]
                    free[link] = max(free.get(link, 0.0), now) + sizes[message][1] / rate
                    arrived[message] = free[link] + trip
                    steps.append(("send", message))
                    issued = True
        _, _, time, then = tasks.pop(task)
        now = max(now, at) + time
        done[task] = now
        steps.append(("task", task))
        for message in then:
            push(message)
    return steps


def ring(p, sign, steps):
    return lax.rem(p + 8 - sign * steps, 4)


def rows8(i, size):
    return pl.ds(pl.multiple_of(i, 8), size)


def over_rows(ref, body):
    if len(ref.shape) == 3:
        lax.fori_loop(0, ref.shape[0], lambda j, _: (body((j,)), 0)[1], 0)
    elif ref.shape[0] == 40:
        lax.fori_loop(0, 5, lambda j, _: (body((rows8(8 * j, 8),)), 0)[1], 0)
    else:
        body((slice(None),))


def add_to(out, a, b):
    def one(i):
        out[i] = (a[i].astype(F32) + b[i].astype(F32)).astype(BF16)

    over_rows(out, one)


LOADS = (6, 5)


def kernel(*refs):
    refs = list(refs)

    def take(n):
        taken = tuple(refs[:n])
        del refs[:n]
        return taken

    terms, weights, ms, vs, outs, mo, vo = (take(3) for _ in range(7))
    r1, r2, r3, held = take(3), take(3), take(3), take(2)
    total, wide, near, mb, vb = take(3), take(3), take(3), take(3), take(3)
    ends, cells, (new, edge) = take(2), take(2), take(2)
    a_send, a_recv, b_send, b_recv, c_send, c_recv, e_send, e_recv = take(8)
    p_send, p_recv, q_send, q_recv, r_send, r_recv = take(6)
    load_sem, in_sem, own_sem, out_sem = take(4)

    me = lax.axis_index("dp")
    at = x, y, z = lax.div(me, 16), lax.rem(lax.div(me, 4), 4), lax.rem(me, 4)

    def towards(axis, sign):
        to = list(at)
        to[axis] = lax.rem(at[axis] + 4 + sign, 4)
        return {"dp": to[0] * 16 + to[1] * 4 + to[2]}

    def cols(w, h):
        return pl.ds(*COLS[w][h])

    def source(w, l, h, block, k):
        a, b, _ = ORDER[w][l][h]
        chunk = ring(at[b], SIGN[l], 1 + k)
        if w < 2:
            i, j = (block, chunk) if a == 0 else (chunk, block)
            return terms[w].at[l, i, j, :, cols(w, h)]
        window = rows8(block * 48, 56)
        return terms[w].at[l, chunk, :, window, cols(w, h)] if b == 0 else terms[w].at[l, :, chunk, window, cols(w, h)]

    def slot(w, h, n):
        n = n % LOADS[w // 2]
        return held[0].at[n, :, pl.ds(0, COLS[w][h][1])] if w < 2 else held[1].at[n, :, :, pl.ds(0, COLS[w][h][1])]

    steps = plan()
    loads = [[task for kind, task in steps if kind == "task" and task[0] == "a" and (task[1] == 2) == down] for down in (False, True)]

    def load(down, n):
        _, w, l, h, t, k = loads[down][n]
        block = ring(at[ORDER[w][l][h][0]], SIGN[l], 2 + t)
        return pltpu.make_async_copy(source(w, l, h, block, k), slot(w, h, n), load_sem.at[down, n % LOADS[down]])

    def part(ref, w, h):
        return ref.at[(slice(None),) * (len(ref.shape) - 1) + (cols(w, h),)]

    def last(w, l, h, t):
        block = ring(at[ORDER[w][l][h][2]], SIGN[l], 2 + t)
        return r2[w].at[l, 2, rows8(block * 8, 16), cols(w, h)] if w < 2 else r2[w].at[l, 2, block, :, cols(w, h)]

    def tiles(block, first):
        return pl.ds(0, 56) if first else rows8(block * 48 + 8, 48)

    def message(name, w, l, h, t, k=0, first=False):
        one, two, three = ORDER[w][l][h]
        s = SIGN[l]
        if name == "a":
            axis, sems = one, (a_send.at[w, l, h, k], a_recv.at[w, l, h, t, k])
            dst = part(r1[w].at[l, t, k], w, h)
            src = source(w, l, h, ring(at[one], s, 1), k) if t == 0 else part(r1[w].at[l, t - 1, k], w, h)
        elif name == "b":
            axis, sems = two, (b_send.at[w, l, h], b_recv.at[w, l, h, t])
            dst = part(r2[w].at[l, t], w, h)
            src = part(r1[w].at[l, 2, 0] if t == 0 else r2[w].at[l, t - 1], w, h)
        elif name == "c":
            axis, sems = three, (c_send.at[w, l, h], c_recv.at[w, l, h, t])
            dst = part(r3[w].at[l, t], w, h)
            src = last(w, l, h, -1) if t == 0 else part(r3[w].at[l, t - 1], w, h)
        elif name == "e":
            axis, s, sems = 2, -1, (e_send.at[l, h], e_recv.at[l, h])
            src, dst = part(new.at[l, pl.ds(0, 8)], w, h), part(edge.at[l], w, h)
        elif name == "p":
            axis, sems = three, (p_send.at[w, l, h], p_recv.at[w, l, h, t])
            block = ring(at[three], s, t)
            if w < 2:
                src = dst = part(ends[w].at[l, block], w, h)
            else:
                i, j = (x, block) if three == 1 else (block, y)
                src = dst = outs[2].at[l, i, j, tiles(z, first), cols(w, h)]
                if t == 0:
                    src = new.at[l, pl.ds(0, 56) if first else pl.ds(8, 48), cols(w, h)]
        elif name == "q":
            axis, sems = two, (q_send.at[w, l, h], q_recv.at[w, l, h, t])
            block = ring(at[two], s, t)
            if w < 2:
                i, j = (x, block) if two == 1 else (block, y)
                src = dst = outs[w].at[l, i, j, :, cols(w, h)]
                if t == 0:
                    src = part(cells[w].at[l], w, h)
            else:
                i, j = (slice(None), block) if two == 1 else (block, slice(None))
                src = dst = outs[2].at[l, i, j, tiles(z, first), cols(w, h)]
        else:
            axis, sems = one, (r_send.at[w, l, h, k], r_recv.at[w, l, h, t, k])
            block, chunk = ring(at[one], s, t), ring(at[two], s, k)
            if w < 2:
                i, j = (block, chunk) if one == 0 else (chunk, block)
                src = dst = outs[w].at[l, i, j, :, cols(w, h)]
                if t == k == 0:
                    src = part(cells[w].at[l], w, h)
            else:
                i, j = (slice(None), chunk) if two == 1 else (chunk, slice(None))
                src = dst = outs[2].at[l, i, j, tiles(block, first), cols(w, h)]
        return pltpu.make_async_remote_copy(
            src_ref=src, dst_ref=dst, send_sem=sems[0], recv_sem=sems[1], device_id=towards(axis, s), device_id_type=MESH
        )

    def each(m, act, coming=False):
        name, w, l, h, t = m[:5]
        if w < 2 or name not in "pqr":
            act(message(*m))
            return
        block = z if name != "r" else ring(z, SIGN[l], t + coming)
        pl.when(block == 0)(lambda: act(message(*m, first=True)))
        pl.when(block != 0)(lambda: act(message(*m)))

    def start(m):
        each(m, lambda copy: copy.start())

    def came(m):
        name, w, l, h, t = m[:5]
        each(m, lambda copy: copy.wait_recv(), coming=True)

    def gone(m):
        each(m, lambda copy: copy.wait_send())

    def inputs():
        for w in range(3):
            yield pltpu.make_async_copy(ms[w], mb[w], in_sem.at[w, 0])
            yield pltpu.make_async_copy(vs[w], vb[w], in_sem.at[w, 1])
            yield pltpu.make_async_copy(weights[w].at[:, x, y, rows8(z * APART[w], WINDOW[w]), :], near[w], in_sem.at[w, 2])

    def own(w, l, h, first=False):
        if w < 2:
            return pltpu.make_async_copy(part(cells[w].at[l], w, h), outs[w].at[l, x, y, :, cols(w, h)], own_sem.at[w, l, h])
        src = new.at[l, pl.ds(0, 56) if first else pl.ds(8, 48), cols(w, h)]
        return pltpu.make_async_copy(src, outs[2].at[l, x, y, tiles(z, first), cols(w, h)], own_sem.at[w, l, h])

    def own_each(w, l, h, act):
        if w < 2:
            act(own(w, l, h))
        else:
            pl.when(z == 0)(lambda: act(own(w, l, h, True)))
            pl.when(z != 0)(lambda: act(own(w, l, h)))

    def optimizer(w, h):
        c = cols(w, h)
        width = COLS[w][h][1]

        def one(r, _):
            row = pl.ds(r + 2 * z, 1)
            g = jnp.concatenate([total[w][l, row, c] for l in range(2)], 0)
            old = jnp.concatenate([wide[w][l, row, c] for l in range(2)], 0)
            m = 0.9 * mb[w][r, :, c] + 0.1 * g
            v = 0.95 * vb[w][r, :, c] + 0.05 * g * g
            step = m * lax.rsqrt(v + 1e-8) + 0.1 * old
            out = old - 0.02 * step
            mb[w][r, :, c] = m
            vb[w][r, :, c] = v
            for l in range(2):
                wide[w][l, row, c] = out[l : l + 1]
            return 0

        lax.fori_loop(0, OWNED[w], one, 0)
        for l in range(2):
            to = ends[w].at[l, z] if w < 2 else new.at[l]
            to[:, c] = wide[w][l, :, c].astype(BF16)

    def join(w, l, h):
        c = cols(w, h)
        row = lax.broadcasted_iota(jnp.int32, (8, COLS[w][h][1]), 0)
        top = [ends[w][l, i, 0:8, c].astype(F32) for i in range(4)]
        low = [ends[w][l, i, 8:16, c].astype(F32) for i in range(4)]
        for i, tile in enumerate([top[0], *(jnp.where(row < 2 * i, low[i - 1], top[i]) for i in (1, 2, 3)), low[3]]):
            cells[w][l, 8 * i : 8 * i + 8, c] = tile.astype(BF16)

    def mend(l, h):
        c = cols(2, h)
        row = lax.broadcasted_iota(jnp.int32, (8, COLS[2][h][1]), 0)
        new[l, 48:56, c] = jnp.where(row < 2 * z + 2, new[l, 48:56, c].astype(F32), edge[l, :, c].astype(F32)).astype(BF16)

    for copy in inputs():
        copy.start()
    for down in range(2):
        for n in range(LOADS[down]):
            load(down, n).start()
    barrier = pltpu.get_barrier_semaphore()
    for axis in range(3):
        for sign in SIGN:
            pl.semaphore_signal(barrier, inc=1, device_id=towards(axis, sign), device_id_type=MESH)
    pl.semaphore_wait(barrier, 6)

    used, begun = [0, 0], False
    flying = {}

    def key(m):
        return (*m[:4], m[5] if len(m) > 5 else 0)

    for kind, task in steps:
        if kind == "send":
            if key(task) in flying:
                gone(flying.pop(key(task)))
            if task[0] == "q" and task[1] == 2 and task[4] == 0:
                own_each(*task[1:4], lambda copy: copy.wait())
            start(task)
            flying[key(task)] = task
            continue
        if not begun:
            for copy in inputs():
                copy.wait()
            for w in range(3):
                for l in range(2):
                    wide[w][l] = near[w][l].astype(F32)
            begun = True
        name, w, *rest = task
        if name == "step":
            optimizer(w, rest[0])
            if rest[0] == len(HALVES) - 1:
                pltpu.make_async_copy(mb[w], mo[w], out_sem.at[w, 0]).start()
                pltpu.make_async_copy(vb[w], vo[w], out_sem.at[w, 1]).start()
            continue
        came(task)
        l, h, t, *k = rest
        if name == "a":
            down = w // 2
            n = used[down]
            used[down] += 1
            load(down, n).wait()
            to = part(r1[w].at[l, t, k[0]], w, h)
            add_to(to, to, slot(w, h, n))
            if n + LOADS[down] < len(loads[down]):
                load(down, n + LOADS[down]).start()
        elif name == "b":
            to = part(r2[w].at[l, t], w, h)
            add_to(to, to, part(r1[w].at[l, 2, t + 1], w, h))
        elif name == "c":
            to = part(r3[w].at[l, t], w, h)
            add_to(to, to, last(w, l, h, t))
            if t == 2:
                total[w][l, :, cols(w, h)] = to[...].astype(F32)
        elif name == "e":
            gone(flying.pop(key(task)))
            mend(l, h)
            own_each(w, l, h, lambda copy: copy.start())
        elif name == "p" and t == 2 and w < 2:
            join(w, l, h)
            own_each(w, l, h, lambda copy: copy.start())
    for task in flying.values():
        gone(task)
    for w, l, h in FLOWS:
        if w < 2:
            own_each(w, l, h, lambda copy: copy.wait())
    for w in range(3):
        pltpu.make_async_copy(mb[w], mo[w], out_sem.at[w, 0]).wait()
        pltpu.make_async_copy(vb[w], vo[w], out_sem.at[w, 1]).wait()


SHAPES = ((2, 4, 4, 40, 3200),) * 2 + ((2, 4, 4, 200, 640),)
MOMENTS = ((10, 2, 3200),) * 2 + ((50, 2, 640),)


def exchanged(*arrays):
    dma, vmem = pltpu.SemaphoreType.DMA, pltpu.VMEM
    flow = len(HALVES)
    cells = ((40, 3200), (40, 3200), (4, 56, 640))
    ring_sems = [dma((3, 2, flow)), dma((3, 2, flow, 3))]
    chunk_sems = [dma((3, 2, flow, 4)), dma((3, 2, flow, 3, 4))]
    windows = [(2, n, width) for n, width in zip(WINDOW, WIDTH, strict=True)]
    return pl.pallas_call(
        kernel,
        out_shape=[jax.ShapeDtypeStruct(s, BF16) for s in SHAPES] + [jax.ShapeDtypeStruct(s, F32) for s in MOMENTS * 2],
        in_specs=[pl.BlockSpec(memory_space=pltpu.HBM)] * 12,
        out_specs=[pl.BlockSpec(memory_space=pl.ANY)] * 9,
        scratch_shapes=[
            *(vmem((2, 3, 4, *c), BF16) for c in cells),
            *(vmem((2, 3, *c), BF16) for c in cells),
            *(vmem((2, 3, *s[1:]), BF16) for s in windows),
            vmem((LOADS[0], 40, COLS[0][0][1]), BF16),
            vmem((LOADS[1], 4, 56, COLS[2][0][1]), BF16),
            *(vmem(s, F32) for s in windows),
            *(vmem(s, F32) for s in windows),
            *(vmem(s, BF16) for s in windows),
            *(vmem(s, F32) for s in MOMENTS * 2),
            *(vmem((2, 4, 16, 3200), BF16),) * 2,
            *(vmem((2, 40, 3200), BF16),) * 2,
            vmem((2, 56, 640), BF16),
            vmem((2, 8, 640), BF16),
            *chunk_sems,
            *ring_sems,
            *ring_sems,
            dma((2, flow)),
            dma((2, flow)),
            *ring_sems,
            *ring_sems,
            *chunk_sems,
            dma((2, max(LOADS))),
            dma((3, 3)),
            dma((3, 2, flow)),
            dma((3, 2)),
        ],
        compiler_params=pltpu.CompilerParams(collective_id=0, has_side_effects=True, vmem_limit_bytes=38 * 2**20),
        name="sum_step_gather",
    )(*arrays)


def put_kernel(*refs):
    ins, outs, sem = refs[:9], refs[9:18], refs[18]
    copies = [pltpu.make_async_copy(a, b, sem.at[i]) for i, (a, b) in enumerate(zip(ins, outs, strict=True))]
    for copy in copies:
        copy.start()
    for copy in copies:
        copy.wait()


def put(arrays):
    return pl.pallas_call(
        put_kernel,
        out_shape=[jax.ShapeDtypeStruct(a.shape, a.dtype) for a in arrays],
        in_specs=[pl.BlockSpec(memory_space=pl.ANY)] * 9,
        out_specs=[pl.BlockSpec(memory_space=pltpu.HBM)] * 9,
        scratch_shapes=[pltpu.SemaphoreType.DMA((9,))],
        compiler_params=pltpu.CompilerParams(vmem_limit_bytes=2**20),
        name="put",
    )(*arrays)


def solution(mesh):
    def step(*arrays):
        terms, weights, m, v = (arrays[i : i + 3] for i in (0, 3, 6, 9))
        cut = [a.reshape(s) for a, s in zip((*terms, *weights), SHAPES * 2, strict=True)]
        moments = [a.transpose(1, 0, 2) for a in (*m, *v)]
        out = put(exchanged(*cut, *moments))
        return (*(o.reshape(w.shape) for o, w in zip(out, weights, strict=False)), *(o.transpose(1, 0, 2) for o in out[3:]))

    all_of, cut = P(None, None, None), P(None, "dp", None)
    return jax.shard_map(
        step,
        mesh=mesh,
        in_specs=(P(("rep", "dp"), None, None, None),) * 3 + (all_of,) * 3 + (cut,) * 6,
        out_specs=(P("rep", None, None),) * 3 + (P("rep", "dp", None),) * 6,
        check_vma=False,
    )
```

time: 609 us -> 263 us (0.43)
  waiting for transfers between devices: 481 us -> 0 us
  Pallas kernels: 0 us -> 250 us
  local copies, waits for them, and re-layouts: 105 us -> 12.3 us
  between operations: 15.2 us -> 0.68 us
  other arithmetic: 7.17 us -> 0 us
    unnamed x5 -> x0, waiting for transfers between devices: 265 us -> none
    pallas_call x0 -> x2, Pallas kernels: none -> 250 us  [the longest x1 241 us: exchanged(): pl.pallas_call(kernel, out_shape=[jax.ShapeDtypeStruct(s, BF16) for s in...]
    all_gather x3 -> x0, waiting for transfers between devices: 215 us -> none  [step(): whole = [lax.all_gather(one[0], 'dp', axis=1, tiled=True) for one in new]]
    unnamed x23 -> x16, local copies, waits for them, and re-layouts: 62.6 us -> 12.3 us
    squeeze x1 -> x0, local copies, waits for them, and re-layouts: 40 us -> none  [step(): t[0]]
    convert_element_type x3 -> x0, other arithmetic: 7.17 us -> none  [adamw(): return ((w - 0.02 * step).astype(jnp.bfloat16), m, v)]
  transfers between devices with their start and end apart: 4 -> 0, of which waited for: 4 -> 0; matrix products, arithmetic and copies ran while one was open for 4% -> 0% of each run, Pallas kernels for 0% -> 0%
where the time goes in v2:
time: 263 us
  Pallas kernels  250 us (95%)
  local copies, waits for them, and re-layouts  12.3 us (5%)
    pallas_call x1, Pallas kernels, exchanged(): pl.pallas_call(kernel, out_shape=[jax.ShapeDtypeStruct(s, BF16) for s in...  241 us
    unnamed x16, local copies, waits for them, and re-layouts  12.3 us
    pallas_call x1, Pallas kernels, put(): pl.pallas_call(put_kernel, out_shape=[jax.ShapeDtypeStruct(a.shape, a.dty...  8.78 us

profile of v2, /device:TPU:0, one launch (start us, length us, event | category | flops | bytes accessed | tf_op | source)
XLA Modules:
  0.0 262.7 jit_solution(15132357187426192526)
XLA Ops:
  0.6 0.0 copy-start.2
  0.7 0.9 copy-done.2
  1.6 0.0 copy-start.3
  1.6 0.9 copy-done.3
  2.5 0.0 copy-start.4
  2.5 0.9 copy-done.4
  3.5 0.0 copy-start.5
  3.5 0.9 copy-done.5
  4.4 0.0 copy-start.6
  4.4 0.9 copy-done.6
  5.4 0.0 copy-start.7
  5.4 0.9 copy-done.7
  6.3 240.9 %sum_step_gather.1 = (bf16[2,4,4,40,3200]{4,3,2,1,0:T(8,128)(2,1)S(1)}, bf16[2,4,4,40,3200]{4,3,2,1,0:T(8,128)(2,1)}, bf16[2,4,4,200,640]{4,3,2,1,0:T(8,128)(2,1...) custom-call(bf16[2,4,4,40,3200]{4,3,2,1,0:T(8,128)(2,1)} %bitcast.27, ...), custom_call_target="tpu_custom_call" | custom-call | tf_op jit(solution)/shard_map/sum_step_gather/pallas_call | solution.py:391
  247.2 0.0 copy-start
  247.2 3.3 %copy-done = bf16[2,4,4,40,3200]{4,3,2,1,0:T(8,128)(2,1)S(1)} copy-done((bf16[2,4,4,40,3200]{4,3,2,1,0:T(8,128)(2,1)S(1)}, bf16[2,4,4,40,3200]{4,3,2,1,0:T(8,128)(2,1)}, u32[]{:S(2)}) %copy-start) | copy-done | bytes 8192024
  250.6 0.0 copy-start.1
  250.6 3.3 %copy-done.1 = bf16[2,4,4,200,640]{4,3,2,1,0:T(8,128)(2,1)S(1)} copy-done((bf16[2,4,4,200,640]{4,3,2,1,0:T(8,128)(2,1)S(1)}, bf16[2,4,4,200,640]{4,3,2,1,0:T(8,128)(2,1)}, u32[]{:S(2)}) %copy-start.1) | copy-done | bytes 8192024
  253.9 8.8 %put.1 = (bf16[2,4,4,40,3200]{4,3,2,1,0:T(8,128)(2,1)}, bf16[2,4,4,40,3200]{4,3,2,1,0:T(8,128)(2,1)}, bf16[2,4,4,200,640]{4,3,2,1,0:T(8,128)(2,1)}, f32[10,2,320...) custom-call(bf16[2,4,4,40,3200]{4,3,2,1,0:T(8,128)(2,1)S(1)} %get-tu, ...), custom_call_target="tpu_custom_call" | custom-call | tf_op jit(solution)/shard_map/put/pallas_call | solution.py:438
Async XLA Ops:
  0.6 0.9 copy-start.2
  1.6 0.9 copy-start.3
  2.5 0.9 copy-start.4
  3.5 0.9 copy-start.5
  4.4 0.9 copy-start.6
  5.4 0.9 copy-start.7
  247.2 3.3 %copy-start = (bf16[2,4,4,40,3200]{4,3,2,1,0:T(8,128)(2,1)S(1)}, bf16[2,4,4,40,3200]{4,3,2,1,0:T(8,128)(2,1)}, u32[]{:S(2)}) copy-start(bf16[2,4,4,40,3200]{4,3,2,1,0:T(8,128)(2,1)} %get-tuple-element.28.refs_1_) | copy-start | bytes 24576004
  250.6 3.3 %copy-start.1 = (bf16[2,4,4,200,640]{4,3,2,1,0:T(8,128)(2,1)S(1)}, bf16[2,4,4,200,640]{4,3,2,1,0:T(8,128)(2,1)}, u32[]{:S(2)}) copy-start(bf16[2,4,4,200,640]{4,3,2,1,0:T(8,128)(2,1)} %get-tuple-element.29.refs_2_) | copy-start | bytes 24576004

commit v3 on v2

v3 whole, which is shorter than its diff:
```python
import jax
import jax.numpy as jnp
from jax import lax
from jax.experimental import pallas as pl
from jax.experimental.pallas import tpu as pltpu
from jax.sharding import PartitionSpec as P

BF16, F32 = jnp.bfloat16, jnp.float32
LOGICAL = pl.DeviceIdType.LOGICAL
SIGN = (1, -1)
COLS = (((0, 1664), (1664, 1536)),) * 2 + (((0, 384), (384, 256)),)
HALVES = LAYERS = (0, 1)
WEIGHTS = AXES = HOPS = (0, 1, 2)
CHUNKS = (0, 1, 2, 3)
DOWN = 2
ALL = slice(None)
IN_HBM, IN_VMEM, ANYWHERE = (pl.BlockSpec(memory_space=space) for space in (pltpu.HBM, pltpu.VMEM, pl.ANY))
XYZ, YXZ, ZXY, ZYX = (0, 1, 2), (1, 0, 2), (2, 0, 1), (2, 1, 0)
ORDER = (((XYZ, XYZ),) * 2, ((YXZ, YXZ),) * 2, ((ZXY, ZYX), (ZYX, ZXY)))
FLOWS = tuple((w, l, h) for h in HALVES for w in WEIGHTS for l in LAYERS)
CELL, OWNED, APART, WINDOW = (40, 40, 200), (10, 10, 50), (8, 8, 48), (16, 16, 56)
WIDTH = (3200, 3200, 640)


def plan():
    ahead, rate, trip = 1.0, 46.6e3, 2.2
    sizes, tasks = {}, {}
    for w, l, h in FLOWS:
        one, two, three = ((axis, l) for axis in ORDER[w][l][h])
        width = COLS[w][h][1] * 2
        whole, back, last = width * (40 if w < DOWN else 224), width * (40 if w < DOWN else 192), width * WINDOW[w]
        add = 5 / 2 / 1024 / 1900
        for t in HOPS:
            on = t < 2
            for k in CHUNKS:
                a = ("a", w, l, h, t, k)
                sizes[a] = (one, whole, 1 + h)
                then = [("a", w, l, h, t + 1, k)] if on else [("b", w, l, h, 0)] if k == 0 else []
                then += [("a", w, l, h + 1, 0, k)] if t == 1 and h + 1 < len(HALVES) else []
                tasks[a] = (a, [], whole * add, then)
                r = ("r", w, l, h, t, k)
                sizes[r] = (one, back, 5 + h)
                tasks[r] = (r, [("q", w, l, h, 2)], 0.05, [("r", w, l, h, t + 1, k)] if on else [])
            b, c, p, q = ((name, w, l, h, t) for name in "bcpq")
            sizes.update({b: (two, whole, 0), c: (three, last, 0), p: (three, last, 0), q: (two, back, 0)})
            tasks[b] = (b, [("a", w, l, h, 2, t + 1)], whole * add, [("b", w, l, h, t + 1)] if on else [("c", w, l, h, 0)])
            tasks[c] = (c, [("b", w, l, h, 2)], last * add, [("c", w, l, h, t + 1)] if on else [])
            tasks[p] = (p, [("step", w, h)], 0.05 if on else 0.4, [("p", w, l, h, t + 1)] if on else [("q", w, l, h, 0), ("r", w, l, h, 0, 0)])
            tasks[q] = (q, [("p", w, l, h, 2)], 0.05, ([("q", w, l, h, t + 1)] if on else []) + [("r", w, l, h, 0, t + 1)])
    for h in HALVES:
        for w in WEIGHTS:
            tasks["step", w, h] = (None, [("c", w, l, h, 2) for l in LAYERS], 1.5, [("p" if w < DOWN else "e", w, l, h, 0) for l in LAYERS])
        for l in LAYERS:
            e = ("e", 2, l, h, 0)
            sizes[e] = ((2, 1), 16 * COLS[2][h][1], 0)
            tasks[e] = (e, [("step", 2, h)], 0.1, [("p", 2, l, h, 0)])
    waiting, free, arrived, done, steps, count = {}, {}, {}, {}, [], 0

    def push(message):
        nonlocal count
        link, _, rank = sizes[message]
        waiting.setdefault(link, []).append((rank, count, message))
        waiting[link].sort()
        count += 1

    for k in CHUNKS:
        for w in WEIGHTS:
            for l in LAYERS:
                push(("a", w, l, 0, 0, k))
    now = 0.0
    while tasks:
        issued = True
        while issued:
            ready = []
            for place, (task, (message, before, _, _)) in enumerate(tasks.items()):
                if (message is None or message in arrived) and all(b in done for b in before):
                    ready.append((max([arrived.get(message, 0.0)] + [done[b] for b in before]), place, task))
            at, _, task = min(ready) if ready else (now, 0, None)
            until, issued = max(now + ahead, at + 1.0), False
            for link in sorted(waiting):
                while waiting[link] and free.get(link, 0.0) < until:
                    message = waiting[link].pop(0)[2]
                    free[link] = max(free.get(link, 0.0), now) + sizes[message][1] / rate
                    arrived[message] = free[link] + trip
                    steps.append(("send", message))
                    issued = True
        _, _, time, then = tasks.pop(task)
        now = max(now, at) + time
        done[task] = now
        steps.append(("task", task))
        for message in then:
            push(message)
    return steps


def rows8(i, size):
    return pl.ds(pl.multiple_of(i, 8), size)


def over_rows(ref, body):
    if len(ref.shape) == 3:
        lax.fori_loop(0, ref.shape[0], lambda j, _: (body((j,)), 0)[1], 0)
    elif ref.shape[0] == 40:
        lax.fori_loop(0, 5, lambda j, _: (body((rows8(8 * j, 8),)), 0)[1], 0)
    else:
        body((ALL,))


def either(first, yes, no):
    def call(act):
        act()

    lax.cond(first, lambda: call(yes), lambda: call(no))


def add_to(out, a, b):
    def one(i):
        out[i] = (a[i].astype(F32) + b[i].astype(F32)).astype(BF16)

    over_rows(out, one)


LOADS = (8, 6)


def kernel(*refs):
    refs = list(refs)

    def take(n):
        taken = tuple(refs[:n])
        del refs[:n]
        return taken

    def halved(n):
        return [take(len(HALVES)) for _ in range(n)]

    terms, weights, ms, vs = (take(3) for _ in range(4))
    outs, mo, vo = halved(3), take(3), take(3)
    r1, r2, r3, held = halved(3), halved(3), halved(3), take(2)
    total, wide, near = take(2), take(2), take(3)
    ends, cells, (new, edge) = halved(2), halved(2), halved(2)
    a_send, a_recv, b_send, b_recv, c_send, c_recv, e_send, e_recv = take(8)
    p_send, p_recv, q_send, q_recv, r_send, r_recv = take(6)
    load_sem, in_sem, own_sem = take(3)

    me = lax.axis_index("dp")
    at = x, y, z = lax.div(me, 16), lax.rem(lax.div(me, 4), 4), lax.rem(me, 4)

    places = [[at[axis]] + [lax.rem(at[axis] + n, 4) for n in (1, 2, 3)] for axis in AXES]
    eights, windows, bands = ([[f(p) for p in places[axis]] for axis in AXES] for f in (lambda p: 8 * p, lambda p: 48 * p, lambda p: 48 * p + 8))
    firsts = [p == 0 for p in places[2]]
    next_to = {}
    for axis in AXES:
        for sign in SIGN:
            to = list(at)
            to[axis] = places[axis][sign % 4]
            next_to[axis, sign] = lax.axis_index("rep") * 64 + to[0] * 16 + to[1] * 4 + to[2]

    def towards(axis, sign):
        return next_to[axis, sign]

    def ring(axis, sign, steps, of=places):
        return of[axis][-sign * steps % 4]

    def number(w, l, h):
        return (w * 2 + l) * len(HALVES) + h

    def cols(w, h):
        return pl.ds(*COLS[w][h])

    def source(w, l, h, steps, k):
        a, b, _ = ORDER[w][l][h]
        chunk = ring(b, SIGN[l], 1 + k)
        if w < DOWN:
            block = ring(a, SIGN[l], steps)
            i, j = (block, chunk) if a == 0 else (chunk, block)
            return terms[w].at[l, i, j, :, cols(w, h)]
        window = rows8(ring(a, SIGN[l], steps, windows), 56)
        return terms[w].at[l, chunk, :, window, cols(w, h)] if b == 0 else terms[w].at[l, :, chunk, window, cols(w, h)]

    def slot(w, h, n):
        n = n % LOADS[w // 2]
        return held[0].at[n, :, pl.ds(0, COLS[w][h][1])] if w < DOWN else held[1].at[n, :, :, pl.ds(0, COLS[w][h][1])]

    steps = plan()
    loads = [[task for kind, task in steps if kind == "task" and task[0] == "a" and (task[1] == DOWN) == down] for down in (False, True)]

    def load(down, n):
        _, w, l, h, t, k = loads[down][n]
        return pltpu.make_async_copy(source(w, l, h, 2 + t, k), slot(w, h, n), load_sem.at[down * LOADS[0] + n % LOADS[down]])

    def spot(refs, w, l, h, t, k=None):
        return refs[w][h].at[l * 3 + t if k is None else l * 12 + t * 4 + k]

    def last(w, l, h, t):
        axis = ORDER[w][l][h][2]
        if w < DOWN:
            return r2[w][h].at[l * 3 + 2, rows8(ring(axis, SIGN[l], 2 + t, eights), 16)]
        return r2[w][h].at[l * 3 + 2, ring(axis, SIGN[l], 2 + t)]

    def tiles(steps, first):
        return pl.ds(0, 56) if first else rows8(bands[2][-steps % 4], 48)

    def message(name, w, l, h, t, k=0, first=False):
        one, two, three = ORDER[w][l][h]
        s, n = SIGN[l], number(w, l, h)
        if name == "a":
            axis, sems = one, (a_send.at[n * 4 + k], a_recv.at[n * 12 + t * 4 + k])
            dst = spot(r1, w, l, h, t, k)
            src = source(w, l, h, 1, k) if t == 0 else spot(r1, w, l, h, t - 1, k)
        elif name == "b":
            axis, sems = two, (b_send.at[n], b_recv.at[n * 3 + t])
            dst = spot(r2, w, l, h, t)
            src = spot(r1, w, l, h, 2, 0) if t == 0 else spot(r2, w, l, h, t - 1)
        elif name == "c":
            axis, sems = three, (c_send.at[n], c_recv.at[n * 3 + t])
            dst = spot(r3, w, l, h, t)
            src = last(w, l, h, -1) if t == 0 else spot(r3, w, l, h, t - 1)
        elif name == "e":
            axis, s, sems = 2, -1, (e_send.at[n - 4 * len(HALVES)], e_recv.at[n - 4 * len(HALVES)])
            src, dst = new[h].at[l, pl.ds(0, 8)], edge[h].at[l]
        elif name == "p":
            axis, sems = three, (p_send.at[n], p_recv.at[n * 3 + t])
            block = ring(three, s, t)
            if w < DOWN:
                src = dst = ends[w][h].at[l, block]
            else:
                i, j = (x, block) if three == 1 else (block, y)
                src = dst = outs[DOWN][h].at[l, i, j, tiles(0, first)]
                if t == 0:
                    src = new[h].at[l, pl.ds(0, 56) if first else pl.ds(8, 48)]
        elif name == "q":
            axis, sems = two, (q_send.at[n], q_recv.at[n * 3 + t])
            block = ring(two, s, t)
            if w < DOWN:
                i, j = (x, block) if two == 1 else (block, y)
                src = dst = outs[w][h].at[l, i, j]
                if t == 0:
                    src = cells[w][h].at[l]
            else:
                i, j = (ALL, block) if two == 1 else (block, ALL)
                src = dst = outs[DOWN][h].at[l, i, j, tiles(0, first)]
        else:
            axis, sems = one, (r_send.at[n * 4 + k], r_recv.at[n * 12 + t * 4 + k])
            block, chunk = ring(one, s, t), ring(two, s, k)
            if w < DOWN:
                i, j = (block, chunk) if one == 0 else (chunk, block)
                src = dst = outs[w][h].at[l, i, j]
                if t == k == 0:
                    src = cells[w][h].at[l]
            else:
                i, j = (ALL, chunk) if two == 1 else (chunk, ALL)
                src = dst = outs[DOWN][h].at[l, i, j, tiles(s * t, first)]
        return pltpu.make_async_remote_copy(
            src_ref=src, dst_ref=dst, send_sem=sems[0], recv_sem=sems[1], device_id=towards(axis, s), device_id_type=LOGICAL
        )

    def each(m, act, coming=False):
        name, w, l, h, t = m[:5]
        if w < DOWN or name not in "pqr":
            act(message(*m))
            return
        first = firsts[0] if name != "r" else ring(0, SIGN[l], t + coming, [firsts])
        either(first, lambda: act(message(*m, first=True)), lambda: act(message(*m)))

    def start(m):
        each(m, lambda copy: copy.start())

    def came(m):
        name, w, l, h, t = m[:5]
        each(m, lambda copy: copy.wait_recv(), coming=True)

    def gone(m):
        each(m, lambda copy: copy.wait_send())

    def inputs():
        for w in WEIGHTS:
            yield pltpu.make_async_copy(weights[w].at[:, x, y, rows8(z * APART[w], WINDOW[w]), :], near[w], in_sem.at[w])

    def own(w, l, h, first=False):
        if w < DOWN:
            return pltpu.make_async_copy(cells[w][h].at[l], outs[w][h].at[l, x, y], own_sem.at[number(w, l, h)])
        src = new[h].at[l, pl.ds(0, 56) if first else pl.ds(8, 48)]
        return pltpu.make_async_copy(src, outs[DOWN][h].at[l, x, y, tiles(0, first)], own_sem.at[number(w, l, h)])

    def own_each(w, l, h, act):
        if w < DOWN:
            act(own(w, l, h))
        else:
            either(firsts[0], lambda: act(own(w, l, h, True)), lambda: act(own(w, l, h)))

    def optimizer(w, h):
        c = cols(w, h)

        grad, weight = (ref.at[:, :, pl.ds(0, COLS[w][h][1])] for ref in (total[w // 2], wide[w // 2]))
        for l in LAYERS:
            grad[l] = r3[w][h][l * 3 + 2].astype(F32)
            weight[l] = near[w][l, :, c].astype(F32)

        def one(r, _):
            row = pl.ds(r + 2 * z, 1)
            g = jnp.concatenate([grad[l, row, :] for l in LAYERS], 0)
            old = jnp.concatenate([weight[l, row, :] for l in LAYERS], 0)
            m = 0.9 * ms[w][r, :, c] + 0.1 * g
            v = 0.95 * vs[w][r, :, c] + 0.05 * g * g
            step = m * lax.rsqrt(v + 1e-8) + 0.1 * old
            out = old - 0.02 * step
            mo[w][r, :, c] = m
            vo[w][r, :, c] = v
            for l in LAYERS:
                weight[l, row, :] = out[l : l + 1]
            return 0

        lax.fori_loop(0, OWNED[w], one, 0)
        for l in LAYERS:
            to = ends[w][h].at[l, z] if w < DOWN else new[h].at[l]
            to[...] = weight[l].astype(BF16)

    def join(w, l, h):
        row = lax.broadcasted_iota(jnp.int32, (8, COLS[w][h][1]), 0)
        top = [ends[w][h][l, i, 0:8].astype(F32) for i in range(4)]
        low = [ends[w][h][l, i, 8:16].astype(F32) for i in range(4)]
        for i, tile in enumerate([top[0], *(jnp.where(row < DOWN * i, low[i - 1], top[i]) for i in (1, 2, 3)), low[3]]):
            cells[w][h][l, 8 * i : 8 * i + 8] = tile.astype(BF16)

    def mend(l, h):
        row = lax.broadcasted_iota(jnp.int32, (8, COLS[2][h][1]), 0)
        new[h][l, 48:56] = jnp.where(row < DOWN * z + 2, new[h][l, 48:56].astype(F32), edge[h][l].astype(F32)).astype(BF16)

    for copy in inputs():
        copy.start()
    for down in range(2):
        for n in range(LOADS[down]):
            load(down, n).start()
    barrier = pltpu.get_barrier_semaphore()
    for axis in AXES:
        for sign in SIGN:
            pl.semaphore_signal(barrier, inc=1, device_id=towards(axis, sign), device_id_type=LOGICAL)
    pl.semaphore_wait(barrier, 6)

    used, begun = [0, 0], False
    flying, staying = {}, {f for f in FLOWS if f[0] == 2}

    def key(m):
        return (*m[:4], m[5] if len(m) > 5 else 0)

    for kind, task in steps:
        if kind == "send":
            if key(task) in flying:
                gone(flying.pop(key(task)))
            if task[0] in "qr" and task[1] == DOWN and task[1:4] in staying:
                staying.remove(task[1:4])
                own_each(*task[1:4], lambda copy: copy.wait())
            start(task)
            flying[key(task)] = task
            continue
        if not begun:
            for copy in inputs():
                copy.wait()
            begun = True
        name, w, *rest = task
        if name == "step":
            optimizer(w, rest[0])
            continue
        came(task)
        l, h, t, *k = rest
        if name == "a":
            down = w // 2
            n = used[down]
            used[down] += 1
            load(down, n).wait()
            to = spot(r1, w, l, h, t, k[0])
            add_to(to, to, slot(w, h, n))
            if n + LOADS[down] < len(loads[down]):
                load(down, n + LOADS[down]).start()
        elif name == "b":
            to = spot(r2, w, l, h, t)
            add_to(to, to, spot(r1, w, l, h, 2, t + 1))
        elif name == "c":
            to = spot(r3, w, l, h, t)
            add_to(to, to, last(w, l, h, t))
        elif name == "e":
            gone(flying.pop(key(task)))
            mend(l, h)
            own_each(w, l, h, lambda copy: copy.start())
        elif name == "p" and t == 2 and w < DOWN:
            join(w, l, h)
            own_each(w, l, h, lambda copy: copy.start())
    for task in flying.values():
        gone(task)
    for w, l, h in FLOWS:
        if w < DOWN:
            own_each(w, l, h, lambda copy: copy.wait())


SHAPES = ((2, 4, 4, 40, 3200),) * 2 + ((2, 4, 4, 200, 640),)
MOMENTS = ((10, 2, 3200),) * 2 + ((50, 2, 640),)


def exchanged(*arrays):
    dma, vmem = pltpu.SemaphoreType.DMA, pltpu.VMEM
    flow = len(HALVES)
    ring_sems = [dma((6 * flow,)), dma((18 * flow,))]
    chunk_sems = [dma((24 * flow,)), dma((72 * flow,))]

    def halved(weights, shape, dtype=BF16):
        return [vmem((*shape(w), COLS[w][h][1]), dtype) for w in weights for h in HALVES]

    everything, wide, down = WEIGHTS, WEIGHTS[:DOWN], WEIGHTS[DOWN:]
    results = [jax.ShapeDtypeStruct((*SHAPES[w][:4], COLS[w][h][1]), BF16) for w in everything for h in HALVES]
    return pl.pallas_call(
        kernel,
        out_shape=results + [jax.ShapeDtypeStruct(s, F32) for s in MOMENTS * 2],
        in_specs=[IN_HBM] * 6 + [IN_VMEM] * 6,
        out_specs=[ANYWHERE] * (3 * flow) + [IN_VMEM] * 6,
        scratch_shapes=[
            *halved(everything, lambda w: (24, *((40,) if w < DOWN else (4, 56)))),
            *halved(everything, lambda w: (6, *((40,) if w < DOWN else (4, 56)))),
            *halved(everything, lambda w: (6, WINDOW[w])),
            vmem((LOADS[0], 40, COLS[0][0][1]), BF16),
            vmem((LOADS[1], 4, 56, COLS[2][0][1]), BF16),
            *(vmem((2, WINDOW[w], COLS[w][0][1]), F32) for w in (0, 2)),
            *(vmem((2, WINDOW[w], COLS[w][0][1]), F32) for w in (0, 2)),
            *(vmem((2, n, width), BF16) for n, width in zip(WINDOW, WIDTH, strict=True)),
            *halved(wide, lambda w: (2, 4, 16)),
            *halved(wide, lambda w: (2, 40)),
            *halved(down, lambda w: (2, 56)),
            *halved(down, lambda w: (2, 8)),
            *chunk_sems,
            *ring_sems,
            *ring_sems,
            dma((2 * flow,)),
            dma((2 * flow,)),
            *ring_sems,
            *ring_sems,
            *chunk_sems,
            dma((sum(LOADS),)),
            dma((3,)),
            dma((6 * flow,)),
        ],
        compiler_params=pltpu.CompilerParams(collective_id=0, has_side_effects=True, vmem_limit_bytes=31 * 2**20),
        name="sum_step_gather",
    )(*arrays)


def put_kernel(*refs):
    n = len(HALVES)
    ins, outs, sem = refs[: 3 * n + 6], refs[3 * n + 6 : -1], refs[-1]
    pairs = [(ins[w * n + h], outs[w].at[:, :, :, :, pl.ds(*COLS[w][h])]) for w in WEIGHTS for h in HALVES]
    pairs += zip(ins[3 * n :], outs[3:], strict=True)
    copies = [pltpu.make_async_copy(a, b, sem.at[i]) for i, (a, b) in enumerate(pairs)]
    for copy in copies:
        copy.start()
    for copy in copies:
        copy.wait()


def put(arrays):
    return pl.pallas_call(
        put_kernel,
        out_shape=[jax.ShapeDtypeStruct(s, BF16) for s in SHAPES] + [jax.ShapeDtypeStruct(s, F32) for s in MOMENTS * 2],
        in_specs=[ANYWHERE] * len(arrays),
        out_specs=[IN_HBM] * 9,
        scratch_shapes=[pltpu.SemaphoreType.DMA((len(arrays),))],
        compiler_params=pltpu.CompilerParams(vmem_limit_bytes=2**20),
        name="put",
    )(*arrays)


def solution(mesh):
    def step(*arrays):
        terms, weights, m, v = (arrays[i : i + 3] for i in (0, 3, 6, 9))
        cut = [a.reshape(s) for a, s in zip((*terms, *weights), SHAPES * 2, strict=True)]
        moments = [a.transpose(1, 0, 2) for a in (*m, *v)]
        out = put(exchanged(*cut, *moments))
        return (*(o.reshape(w.shape) for o, w in zip(out, weights, strict=False)), *(o.transpose(1, 0, 2) for o in out[3:]))

    all_of, cut = P(None, None, None), P(None, "dp", None)
    return jax.shard_map(
        step,
        mesh=mesh,
        in_specs=(P(("rep", "dp"), None, None, None),) * 3 + (all_of,) * 3 + (cut,) * 6,
        out_specs=(P("rep", None, None),) * 3 + (P("rep", "dp", None),) * 6,
        check_vma=False,
    )
```

time: 263 us -> 222 us (0.84)
  Pallas kernels: 250 us -> 213 us
  local copies, waits for them, and re-layouts: 12.3 us -> 8.06 us
    pallas_call x2, Pallas kernels: 250 us -> 213 us  [the longest x1 204 us: exchanged(): pl.pallas_call(kernel, out_shape=results + [jax.ShapeDtypeStruct(s, F32)...]
    unnamed x16 -> x14, local copies, waits for them, and re-layouts: 12.3 us -> 8.06 us
where the time goes in v3:
time: 222 us
  Pallas kernels  213 us (96%)
  local copies, waits for them, and re-layouts  8.06 us (4%)
    pallas_call x1, Pallas kernels, exchanged(): pl.pallas_call(kernel, out_shape=results + [jax.ShapeDtypeStruct(s, F32)...  204 us
    pallas_call x1, Pallas kernels, put(): pl.pallas_call(put_kernel, out_shape=[jax.ShapeDtypeStruct(s, BF16) for s...  8.7 us
    unnamed x14, local copies, waits for them, and re-layouts  8.06 us

profile of v3, /device:TPU:0, one launch (start us, length us, event | category | flops | bytes accessed | tf_op | source)
XLA Modules:
  0.0 221.7 jit_solution(8153353450714231055)
XLA Ops:
  0.6 0.0 copy-start.1
  0.7 0.9 copy-done.1
  1.6 0.0 copy-start.2
  1.6 0.9 copy-done.2
  2.5 0.0 copy-start.3
  2.5 0.9 copy-done.3
  3.5 0.0 copy-start.4
  3.5 0.9 copy-done.4
  4.4 0.0 copy-start.5
  4.4 0.9 copy-done.5
  5.4 0.0 copy-start.6
  5.4 0.9 copy-done.6
  6.3 204.2 %sum_step_gather.1 = (bf16[2,4,4,40,1664]{4,3,2,1,0:T(8,128)(2,1)S(1)}, bf16[2,4,4,40,1536]{4,3,2,1,0:T(8,128)(2,1)S(1)}, bf16[2,4,4,40,1664]{4,3,2,1,0:T(8,128)...) custom-call(bf16[2,4,4,40,3200]{4,3,2,1,0:T(8,128)(2,1)} %bitcast.27, ...), custom_call_target="tpu_custom_call" | custom-call | tf_op jit(solution)/shard_map/sum_step_gather/pallas_call | solution.py:411
  210.6 0.0 copy-start
  210.6 2.4 %copy-done = bf16[2,4,4,200,384]{4,3,2,1,0:T(8,128)(2,1)S(1)} copy-done((bf16[2,4,4,200,384]{4,3,2,1,0:T(8,128)(2,1)S(1)}, bf16[2,4,4,200,384]{4,3,2,1,0:T(8,128)(2,1)}, u32[]{:S(2)}) %copy-start) | copy-done | bytes 4915224
  213.0 8.7 %put.1 = (bf16[2,4,4,40,3200]{4,3,2,1,0:T(8,128)(2,1)}, bf16[2,4,4,40,3200]{4,3,2,1,0:T(8,128)(2,1)}, bf16[2,4,4,200,640]{4,3,2,1,0:T(8,128)(2,1)}, f32[10,2,320...) custom-call(bf16[2,4,4,40,1664]{4,3,2,1,0:T(8,128)(2,1)S(1)} %get-tu, ...), custom_call_target="tpu_custom_call" | custom-call | tf_op jit(solution)/shard_map/put/pallas_call | solution.py:459
Async XLA Ops:
  0.6 0.9 copy-start.1
  1.6 0.9 copy-start.2
  2.5 0.9 copy-start.3
  3.5 0.9 copy-start.4
  4.4 0.9 copy-start.5
  5.4 0.9 copy-start.6
  210.6 2.4 %copy-start = (bf16[2,4,4,200,384]{4,3,2,1,0:T(8,128)(2,1)S(1)}, bf16[2,4,4,200,384]{4,3,2,1,0:T(8,128)(2,1)}, u32[]{:S(2)}) copy-start(bf16[2,4,4,200,384]{4,3,2,1,0:T(8,128)(2,1)} %get-tuple-element.34.refs_4_) | copy-start | bytes 14745604

commit v4 on v3

--- a/solution.py
+++ b/solution.py
@@ -23,7 +23,7 @@
 
 
 def plan():
-    ahead, rate, trip = 1.0, 46.6e3, 2.2
+    ahead, rate, trip = 1.0, 46.6e3, 3.0
     sizes, tasks = {}, {}
     for w, l, h in FLOWS:
         one, two, three = ((axis, l) for axis in ORDER[w][l][h])
@@ -137,7 +137,7 @@
     terms, weights, ms, vs = (take(3) for _ in range(4))
     outs, mo, vo = halved(3), take(3), take(3)
     r1, r2, r3, held = halved(3), halved(3), halved(3), take(2)
-    total, wide, near = take(2), take(2), take(3)
+    total, wide, near, mb, vb = take(2), take(2), take(3), take(3), take(3)
     ends, cells, (new, edge) = halved(2), halved(2), halved(2)
     a_send, a_recv, b_send, b_recv, c_send, c_recv, e_send, e_recv = take(8)
     p_send, p_recv, q_send, q_recv, r_send, r_recv = take(6)
@@ -276,6 +276,8 @@
     def inputs():
         for w in WEIGHTS:
             yield pltpu.make_async_copy(weights[w].at[:, x, y, rows8(z * APART[w], WINDOW[w]), :], near[w], in_sem.at[w])
+            yield pltpu.make_async_copy(ms[w], mb[w], in_sem.at[w + 3])
+            yield pltpu.make_async_copy(vs[w], vb[w], in_sem.at[w + 6])
 
     def own(w, l, h, first=False):
         if w < DOWN:
@@ -301,8 +303,8 @@
             row = pl.ds(r + 2 * z, 1)
             g = jnp.concatenate([grad[l, row, :] for l in LAYERS], 0)
             old = jnp.concatenate([weight[l, row, :] for l in LAYERS], 0)
-            m = 0.9 * ms[w][r, :, c] + 0.1 * g
-            v = 0.95 * vs[w][r, :, c] + 0.05 * g * g
+            m = 0.9 * mb[w][r, :, c] + 0.1 * g
+            v = 0.95 * vb[w][r, :, c] + 0.05 * g * g
             step = m * lax.rsqrt(v + 1e-8) + 0.1 * old
             out = old - 0.02 * step
             mo[w][r, :, c] = m
@@ -407,11 +409,11 @@
         return [vmem((*shape(w), COLS[w][h][1]), dtype) for w in weights for h in HALVES]
 
     everything, wide, down = WEIGHTS, WEIGHTS[:DOWN], WEIGHTS[DOWN:]
-    results = [jax.ShapeDtypeStruct((*SHAPES[w][:4], COLS[w][h][1]), BF16) for w in everything for h in HALVES]
+    results = [vmem((*SHAPES[w][:4], COLS[w][h][1]), BF16) for w in everything for h in HALVES]
     return pl.pallas_call(
         kernel,
-        out_shape=results + [jax.ShapeDtypeStruct(s, F32) for s in MOMENTS * 2],
-        in_specs=[IN_HBM] * 6 + [IN_VMEM] * 6,
+        out_shape=results + [vmem(s, F32) for s in MOMENTS * 2],
+        in_specs=[IN_HBM] * 12,
         out_specs=[ANYWHERE] * (3 * flow) + [IN_VMEM] * 6,
         scratch_shapes=[
             *halved(everything, lambda w: (24, *((40,) if w < DOWN else (4, 56)))),
@@ -422,6 +424,7 @@
             *(vmem((2, WINDOW[w], COLS[w][0][1]), F32) for w in (0, 2)),
             *(vmem((2, WINDOW[w], COLS[w][0][1]), F32) for w in (0, 2)),
             *(vmem((2, n, width), BF16) for n, width in zip(WINDOW, WIDTH, strict=True)),
+            *(vmem(s, F32) for s in MOMENTS * 2),
             *halved(wide, lambda w: (2, 4, 16)),
             *halved(wide, lambda w: (2, 40)),
             *halved(down, lambda w: (2, 56)),
@@ -435,10 +438,10 @@
             *ring_sems,
             *chunk_sems,
             dma((sum(LOADS),)),
-            dma((3,)),
+            dma((9,)),
             dma((6 * flow,)),
         ],
-        compiler_params=pltpu.CompilerParams(collective_id=0, has_side_effects=True, vmem_limit_bytes=31 * 2**20),
+        compiler_params=pltpu.CompilerParams(collective_id=0, has_side_effects=True, vmem_limit_bytes=33 * 2**20),
         name="sum_step_gather",
     )(*arrays)
 
@@ -471,7 +474,7 @@
     def step(*arrays):
         terms, weights, m, v = (arrays[i : i + 3] for i in (0, 3, 6, 9))
         cut = [a.reshape(s) for a, s in zip((*terms, *weights), SHAPES * 2, strict=True)]
-        moments = [a.transpose(1, 0, 2) for a in (*m, *v)]
+        moments = [pltpu.with_memory_space_constraint(a.transpose(1, 0, 2), pltpu.HBM) for a in (*m, *v)]
         out = put(exchanged(*cut, *moments))
         return (*(o.reshape(w.shape) for o, w in zip(out, weights, strict=False)), *(o.transpose(1, 0, 2) for o in out[3:]))
 

time: 222 us -> 214 us (0.964)
  local copies, waits for them, and re-layouts: 8.06 us -> 0 us
    unnamed x14 -> x0, local copies, waits for them, and re-layouts: 8.06 us -> none
where the time goes in v4:
time: 214 us; the launch traced here: 213 us
  Pallas kernels  213 us (100%)
    pallas_call x1, Pallas kernels, exchanged(): pl.pallas_call(kernel, out_shape=results + [vmem(s, F32) for s in MOMENTS...  204 us
    pallas_call x1, Pallas kernels, put(): pl.pallas_call(put_kernel, out_shape=[jax.ShapeDtypeStruct(s, BF16) for s...  8.71 us

profile of v4, /device:TPU:0, one launch (start us, length us, event | category | flops | bytes accessed | tf_op | source)
XLA Modules:
  0.0 213.4 jit_solution(6557400424489279261)
XLA Ops:
  0.6 204.0 %sum_step_gather.1 = (bf16[2,4,4,40,1664]{4,3,2,1,0:T(8,128)(2,1)S(1)}, bf16[2,4,4,40,1536]{4,3,2,1,0:T(8,128)(2,1)S(1)}, bf16[2,4,4,40,1664]{4,3,2,1,0:T(8,128)...) custom-call(bf16[2,4,4,40,3200]{4,3,2,1,0:T(8,128)(2,1)} %bitcast.21, ...), custom_call_target="tpu_custom_call" | custom-call | tf_op jit(solution)/shard_map/sum_step_gather/pallas_call | solution.py:413
  204.7 8.7 %put.1 = (bf16[2,4,4,40,3200]{4,3,2,1,0:T(8,128)(2,1)}, bf16[2,4,4,40,3200]{4,3,2,1,0:T(8,128)(2,1)}, bf16[2,4,4,200,640]{4,3,2,1,0:T(8,128)(2,1)}, f32[10,2,320...) custom-call(bf16[2,4,4,40,1664]{4,3,2,1,0:T(8,128)(2,1)S(1)} %get-tu, ...), custom_call_target="tpu_custom_call" | custom-call | tf_op jit(solution)/shard_map/put/pallas_call | solution.py:462

commit v5 on v4

--- a/solution.py
+++ b/solution.py
@@ -8,45 +8,58 @@
 BF16, F32 = jnp.bfloat16, jnp.float32
 LOGICAL = pl.DeviceIdType.LOGICAL
 SIGN = (1, -1)
-COLS = (((0, 1664), (1664, 1536)),) * 2 + (((0, 384), (384, 256)),)
+COLS = (((0, 1536), (1536, 1664)),) * 2 + (((0, 384), (384, 256)),)
 HALVES = LAYERS = (0, 1)
 WEIGHTS = AXES = HOPS = (0, 1, 2)
 CHUNKS = (0, 1, 2, 3)
 DOWN = 2
+CELLS = (4,)
 ALL = slice(None)
 IN_HBM, IN_VMEM, ANYWHERE = (pl.BlockSpec(memory_space=space) for space in (pltpu.HBM, pltpu.VMEM, pl.ANY))
 XYZ, YXZ, ZXY, ZYX = (0, 1, 2), (1, 0, 2), (2, 0, 1), (2, 1, 0)
-ORDER = (((XYZ, XYZ),) * 2, ((YXZ, YXZ),) * 2, ((ZXY, ZYX), (ZYX, ZXY)))
+ORDER = (((XYZ, XYZ),) * 2, ((YXZ, YXZ),) * 2, ((ZXY, ZYX),) * 2)
 FLOWS = tuple((w, l, h) for h in HALVES for w in WEIGHTS for l in LAYERS)
 CELL, OWNED, APART, WINDOW = (40, 40, 200), (10, 10, 50), (8, 8, 48), (16, 16, 56)
 WIDTH = (3200, 3200, 640)
+MOST = tuple(max(width for _, width in halves) for halves in COLS)
+
+
+def cross(w, h):
+    return w == 1 and h == 0
+
+
+def back(w, l, h):
+    one, two, three = ORDER[w][l][h]
+    return (one, three, two) if cross(w, h) else (one, two, three)
 
 
 def plan():
-    ahead, rate, trip = 1.0, 46.6e3, 3.0
+    ahead, rate, trip, little = 0.5, 44.0e3, 3.0, 0.05
     sizes, tasks = {}, {}
     for w, l, h in FLOWS:
         one, two, three = ((axis, l) for axis in ORDER[w][l][h])
+        _, late, early = ((axis, l) for axis in back(w, l, h))
         width = COLS[w][h][1] * 2
-        whole, back, last = width * (40 if w < DOWN else 224), width * (40 if w < DOWN else 192), width * WINDOW[w]
-        add = 5 / 2 / 1024 / 1900
+        whole, part, last = width * (40 if w < DOWN else 224), width * (40 if w < DOWN else 192), width * WINDOW[w]
+        add, four = 5 / 2 / 1024 / 1900, cross(w, h)
         for t in HOPS:
             on = t < 2
             for k in CHUNKS:
                 a = ("a", w, l, h, t, k)
-                sizes[a] = (one, whole, 1 + h)
+                sizes[a] = (one, whole, 1 + 0.5 * h - 0.1 * t)
                 then = [("a", w, l, h, t + 1, k)] if on else [("b", w, l, h, 0)] if k == 0 else []
-                then += [("a", w, l, h + 1, 0, k)] if t == 1 and h + 1 < len(HALVES) else []
+                then += [("a", w, l, h + 1, 0, k)] if t == 2 and h + 1 < len(HALVES) else []
                 tasks[a] = (a, [], whole * add, then)
                 r = ("r", w, l, h, t, k)
-                sizes[r] = (one, back, 5 + h)
-                tasks[r] = (r, [("q", w, l, h, 2)], 0.05, [("r", w, l, h, t + 1, k)] if on else [])
+                sizes[r] = (one, part, 5 + -1 * h + 0 * t)
+                tasks[r] = (r, [("q", w, l, h, 2)], little, [("r", w, l, h, t + 1, k)] if on else [])
             b, c, p, q = ((name, w, l, h, t) for name in "bcpq")
-            sizes.update({b: (two, whole, 0), c: (three, last, 0), p: (three, last, 0), q: (two, back, 0)})
+            sizes.update({b: (two, whole, 0), c: (three, last, 0), p: (early, last, -2), q: (late, width * 64 if four else part, 2 - 2 * h)})
             tasks[b] = (b, [("a", w, l, h, 2, t + 1)], whole * add, [("b", w, l, h, t + 1)] if on else [("c", w, l, h, 0)])
             tasks[c] = (c, [("b", w, l, h, 2)], last * add, [("c", w, l, h, t + 1)] if on else [])
-            tasks[p] = (p, [("step", w, h)], 0.05 if on else 0.4, [("p", w, l, h, t + 1)] if on else [("q", w, l, h, 0), ("r", w, l, h, 0, 0)])
-            tasks[q] = (q, [("p", w, l, h, 2)], 0.05, ([("q", w, l, h, t + 1)] if on else []) + [("r", w, l, h, 0, t + 1)])
+            tasks[p] = (p, [("step", w, h)], little if on else 0.4, [("p", w, l, h, t + 1)] if on else [("q", w, l, h, 0)] + [("r", w, l, h, 0, 0)] * (not four))
+            then = [("r", w, l, h, 0, k) for k in CHUNKS if t == 2] if four else [("r", w, l, h, 0, t + 1)]
+            tasks[q] = (q, [("p", w, l, h, 2)], little, ([("q", w, l, h, t + 1)] if on else []) + then)
     for h in HALVES:
         for w in WEIGHTS:
             tasks["step", w, h] = (None, [("c", w, l, h, 2) for l in LAYERS], 1.5, [("p" if w < DOWN else "e", w, l, h, 0) for l in LAYERS])
@@ -75,8 +88,8 @@
             for place, (task, (message, before, _, _)) in enumerate(tasks.items()):
                 if (message is None or message in arrived) and all(b in done for b in before):
                     ready.append((max([arrived.get(message, 0.0)] + [done[b] for b in before]), place, task))
-            at, _, task = min(ready) if ready else (now, 0, None)
-            until, issued = max(now + ahead, at + 1.0), False
+            at, _, task = min(ready) if ready else (now + 9, 0, None)
+            until, issued = max(now + ahead, at + 0.3), False
             for link in sorted(waiting):
                 while waiting[link] and free.get(link, 0.0) < until:
                     message = waiting[link].pop(0)[2]
@@ -138,7 +151,7 @@
     outs, mo, vo = halved(3), take(3), take(3)
     r1, r2, r3, held = halved(3), halved(3), halved(3), take(2)
     total, wide, near, mb, vb = take(2), take(2), take(3), take(3), take(3)
-    ends, cells, (new, edge) = halved(2), halved(2), halved(2)
+    ends, (new, edge) = halved(2), halved(2)
     a_send, a_recv, b_send, b_recv, c_send, c_recv, e_send, e_recv = take(8)
     p_send, p_recv, q_send, q_recv, r_send, r_recv = take(6)
     load_sem, in_sem, own_sem = take(3)
@@ -170,7 +183,7 @@
 
     def source(w, l, h, steps, k):
         a, b, _ = ORDER[w][l][h]
-        chunk = ring(b, SIGN[l], 1 + k)
+        chunk = ring(1 - a if w < DOWN else b, SIGN[l], 1 + k)
         if w < DOWN:
             block = ring(a, SIGN[l], steps)
             i, j = (block, chunk) if a == 0 else (chunk, block)
@@ -195,14 +208,14 @@
     def last(w, l, h, t):
         axis = ORDER[w][l][h][2]
         if w < DOWN:
-            return r2[w][h].at[l * 3 + 2, rows8(ring(axis, SIGN[l], 2 + t, eights), 16)]
+            return r2[w][h].at[l * 3 + 2, rows8(ring(axis, SIGN[l], t + 2, eights), 16)]
         return r2[w][h].at[l * 3 + 2, ring(axis, SIGN[l], 2 + t)]
 
     def tiles(steps, first):
         return pl.ds(0, 56) if first else rows8(bands[2][-steps % 4], 48)
 
     def message(name, w, l, h, t, k=0, first=False):
-        one, two, three = ORDER[w][l][h]
+        one, two, three = back(w, l, h) if name in "pqr" else ORDER[w][l][h]
         s, n = SIGN[l], number(w, l, h)
         if name == "a":
             axis, sems = one, (a_send.at[n * 4 + k], a_recv.at[n * 12 + t * 4 + k])
@@ -217,13 +230,13 @@
             dst = spot(r3, w, l, h, t)
             src = last(w, l, h, -1) if t == 0 else spot(r3, w, l, h, t - 1)
         elif name == "e":
-            axis, s, sems = 2, -1, (e_send.at[n - 4 * len(HALVES)], e_recv.at[n - 4 * len(HALVES)])
+            axis, s, sems = 2, -1, (e_send.at[n], e_recv.at[n])
             src, dst = new[h].at[l, pl.ds(0, 8)], edge[h].at[l]
         elif name == "p":
             axis, sems = three, (p_send.at[n], p_recv.at[n * 3 + t])
             block = ring(three, s, t)
             if w < DOWN:
-                src = dst = ends[w][h].at[l, block]
+                src = dst = ends[w][h].at[l, block, z] if cross(w, h) else ends[w][h].at[l, block]
             else:
                 i, j = (x, block) if three == 1 else (block, y)
                 src = dst = outs[DOWN][h].at[l, i, j, tiles(0, first)]
@@ -232,22 +245,20 @@
         elif name == "q":
             axis, sems = two, (q_send.at[n], q_recv.at[n * 3 + t])
             block = ring(two, s, t)
-            if w < DOWN:
+            if cross(w, h):
+                src = dst = ends[w][h].at[l, :, block]
+            elif w < DOWN:
                 i, j = (x, block) if two == 1 else (block, y)
                 src = dst = outs[w][h].at[l, i, j]
-                if t == 0:
-                    src = cells[w][h].at[l]
             else:
                 i, j = (ALL, block) if two == 1 else (block, ALL)
                 src = dst = outs[DOWN][h].at[l, i, j, tiles(0, first)]
         else:
             axis, sems = one, (r_send.at[n * 4 + k], r_recv.at[n * 12 + t * 4 + k])
-            block, chunk = ring(one, s, t), ring(two, s, k)
+            block, chunk = ring(one, s, t), ring(1 - one if w < DOWN else two, s, k)
             if w < DOWN:
                 i, j = (block, chunk) if one == 0 else (chunk, block)
                 src = dst = outs[w][h].at[l, i, j]
-                if t == k == 0:
-                    src = cells[w][h].at[l]
             else:
                 i, j = (ALL, chunk) if two == 1 else (chunk, ALL)
                 src = dst = outs[DOWN][h].at[l, i, j, tiles(s * t, first)]
@@ -279,17 +290,12 @@
             yield pltpu.make_async_copy(ms[w], mb[w], in_sem.at[w + 3])
             yield pltpu.make_async_copy(vs[w], vb[w], in_sem.at[w + 6])
 
-    def own(w, l, h, first=False):
-        if w < DOWN:
-            return pltpu.make_async_copy(cells[w][h].at[l], outs[w][h].at[l, x, y], own_sem.at[number(w, l, h)])
-        src = new[h].at[l, pl.ds(0, 56) if first else pl.ds(8, 48)]
-        return pltpu.make_async_copy(src, outs[DOWN][h].at[l, x, y, tiles(0, first)], own_sem.at[number(w, l, h)])
-
-    def own_each(w, l, h, act):
-        if w < DOWN:
-            act(own(w, l, h))
-        else:
-            either(firsts[0], lambda: act(own(w, l, h, True)), lambda: act(own(w, l, h)))
+    def own(l, h, act):
+        def copy(first):
+            src = new[h].at[l, pl.ds(0, 56) if first else pl.ds(8, 48)]
+            return pltpu.make_async_copy(src, outs[DOWN][h].at[l, x, y, tiles(0, first)], own_sem.at[l * len(HALVES) + h])
+
+        either(firsts[0], lambda: act(copy(True)), lambda: act(copy(False)))
 
     def optimizer(w, h):
         c = cols(w, h)
@@ -315,15 +321,26 @@
 
         lax.fori_loop(0, OWNED[w], one, 0)
         for l in LAYERS:
-            to = ends[w][h].at[l, z] if w < DOWN else new[h].at[l]
+            to = ends[w][h].at[(l, y if w == 0 else x, z) if cross(w, h) else (l, z)] if w < DOWN else new[h].at[l]
             to[...] = weight[l].astype(BF16)
 
     def join(w, l, h):
         row = lax.broadcasted_iota(jnp.int32, (8, COLS[w][h][1]), 0)
-        top = [ends[w][h][l, i, 0:8].astype(F32) for i in range(4)]
-        low = [ends[w][h][l, i, 8:16].astype(F32) for i in range(4)]
-        for i, tile in enumerate([top[0], *(jnp.where(row < DOWN * i, low[i - 1], top[i]) for i in (1, 2, 3)), low[3]]):
-            cells[w][h][l, 8 * i : 8 * i + 8] = tile.astype(BF16)
+
+        def one(windows, *cell):
+            top = [windows[i, 0:8].astype(F32) for i in CHUNKS]
+            low = [windows[i, 8:16].astype(F32) for i in CHUNKS]
+            for i, tile in enumerate([top[0], *(jnp.where(row < 2 * i, low[i - 1], top[i]) for i in CHUNKS[1:]), low[3]]):
+                outs[w][h][l, *cell, 8 * i : 8 * i + 8] = tile.astype(BF16)
+
+        def some(n, _):
+            one(ends[w][h].at[l, n], *((x, n) if ORDER[w][l][h][0] == 0 else (n, y)))
+            return 0
+
+        if cross(w, h):
+            lax.fori_loop(0, 4, some, 0)
+        else:
+            one(ends[w][h].at[l], x, y)
 
     def mend(l, h):
         row = lax.broadcasted_iota(jnp.int32, (8, COLS[2][h][1]), 0)
@@ -350,9 +367,9 @@
         if kind == "send":
             if key(task) in flying:
                 gone(flying.pop(key(task)))
-            if task[0] in "qr" and task[1] == DOWN and task[1:4] in staying:
+            if task[0] in "qr" and task[1:4] in staying:
                 staying.remove(task[1:4])
-                own_each(*task[1:4], lambda copy: copy.wait())
+                own(*task[2:4], lambda copy: copy.wait())
             start(task)
             flying[key(task)] = task
             continue
@@ -384,15 +401,11 @@
         elif name == "e":
             gone(flying.pop(key(task)))
             mend(l, h)
-            own_each(w, l, h, lambda copy: copy.start())
-        elif name == "p" and t == 2 and w < DOWN:
+            own(l, h, lambda copy: copy.start())
+        elif name == ("q" if cross(w, h) else "p") and t == 2 and w < DOWN:
             join(w, l, h)
-            own_each(w, l, h, lambda copy: copy.start())
     for task in flying.values():
         gone(task)
-    for w, l, h in FLOWS:
-        if w < DOWN:
-            own_each(w, l, h, lambda copy: copy.wait())
 
 
 SHAPES = ((2, 4, 4, 40, 3200),) * 2 + ((2, 4, 4, 200, 640),)
@@ -402,11 +415,10 @@
 def exchanged(*arrays):
     dma, vmem = pltpu.SemaphoreType.DMA, pltpu.VMEM
     flow = len(HALVES)
-    ring_sems = [dma((6 * flow,)), dma((18 * flow,))]
-    chunk_sems = [dma((24 * flow,)), dma((72 * flow,))]
+    ring_sems, chunk_sems = ([dma((n * len(FLOWS),)) for n in (each, 3 * each)] for each in (1, 4))
 
     def halved(weights, shape, dtype=BF16):
-        return [vmem((*shape(w), COLS[w][h][1]), dtype) for w in weights for h in HALVES]
+        return [vmem((*shape(w, cross(w, h)), COLS[w][h][1]), dtype) for w in weights for h in HALVES]
 
     everything, wide, down = WEIGHTS, WEIGHTS[:DOWN], WEIGHTS[DOWN:]
     results = [vmem((*SHAPES[w][:4], COLS[w][h][1]), BF16) for w in everything for h in HALVES]
@@ -414,34 +426,32 @@
         kernel,
         out_shape=results + [vmem(s, F32) for s in MOMENTS * 2],
         in_specs=[IN_HBM] * 12,
-        out_specs=[ANYWHERE] * (3 * flow) + [IN_VMEM] * 6,
+        out_specs=[IN_VMEM] * (3 * flow + 6),
         scratch_shapes=[
-            *halved(everything, lambda w: (24, *((40,) if w < DOWN else (4, 56)))),
-            *halved(everything, lambda w: (6, *((40,) if w < DOWN else (4, 56)))),
-            *halved(everything, lambda w: (6, WINDOW[w])),
-            vmem((LOADS[0], 40, COLS[0][0][1]), BF16),
-            vmem((LOADS[1], 4, 56, COLS[2][0][1]), BF16),
-            *(vmem((2, WINDOW[w], COLS[w][0][1]), F32) for w in (0, 2)),
-            *(vmem((2, WINDOW[w], COLS[w][0][1]), F32) for w in (0, 2)),
+            *halved(everything, lambda w, four: (24, *((40,) if w < DOWN else (4, 56)))),
+            *halved(everything, lambda w, four: (6, *((40,) if w < DOWN else (4, 56)))),
+            *halved(everything, lambda w, four: (6, WINDOW[w])),
+            vmem((LOADS[0], 40, MOST[0]), BF16),
+            vmem((LOADS[1], 4, 56, MOST[DOWN]), BF16),
+            *(vmem((2, WINDOW[w], MOST[w]), F32) for w in (0, 2)),
+            *(vmem((2, WINDOW[w], MOST[w]), F32) for w in (0, 2)),
             *(vmem((2, n, width), BF16) for n, width in zip(WINDOW, WIDTH, strict=True)),
             *(vmem(s, F32) for s in MOMENTS * 2),
-            *halved(wide, lambda w: (2, 4, 16)),
-            *halved(wide, lambda w: (2, 40)),
-            *halved(down, lambda w: (2, 56)),
-            *halved(down, lambda w: (2, 8)),
+            *halved(wide, lambda w, four: (2, *CELLS[:four], 4, 16)),
+            *halved(down, lambda w, four: (2, 56)),
+            *halved(down, lambda w, four: (2, 8)),
             *chunk_sems,
             *ring_sems,
             *ring_sems,
-            dma((2 * flow,)),
-            dma((2 * flow,)),
+            *ring_sems,
             *ring_sems,
             *ring_sems,
             *chunk_sems,
             dma((sum(LOADS),)),
             dma((9,)),
-            dma((6 * flow,)),
+            dma((len(FLOWS),)),
         ],
-        compiler_params=pltpu.CompilerParams(collective_id=0, has_side_effects=True, vmem_limit_bytes=33 * 2**20),
+        compiler_params=pltpu.CompilerParams(collective_id=0, has_side_effects=True, vmem_limit_bytes=35 * 2**20),
         name="sum_step_gather",
     )(*arrays)
 

time: 214 us -> 212 us (level)
  no operation moved by 1% of the time
where the time goes in v5:
time: 212 us
  Pallas kernels  212 us (100%)
    pallas_call x1, Pallas kernels, exchanged(): pl.pallas_call(kernel, out_shape=results + [vmem(s, F32) for s in MOMENTS...  203 us
    pallas_call x1, Pallas kernels, put(): pl.pallas_call(put_kernel, out_shape=[jax.ShapeDtypeStruct(s, BF16) for s...  8.82 us

profile of v5, /device:TPU:0, one launch (start us, length us, event | category | flops | bytes accessed | tf_op | source)
XLA Modules:
  0.0 212.2 jit_solution(459591177976448659)
XLA Ops:
  0.6 202.7 %sum_step_gather.1 = (bf16[2,4,4,40,1536]{4,3,2,1,0:T(8,128)(2,1)S(1)}, bf16[2,4,4,40,1664]{4,3,2,1,0:T(8,128)(2,1)S(1)}, bf16[2,4,4,40,1536]{4,3,2,1,0:T(8,128)...) custom-call(bf16[2,4,4,40,3200]{4,3,2,1,0:T(8,128)(2,1)} %bitcast.21, ...), custom_call_target="tpu_custom_call" | custom-call | tf_op jit(solution)/shard_map/sum_step_gather/pallas_call | solution.py:425
  203.4 8.8 %put.1 = (bf16[2,4,4,40,3200]{4,3,2,1,0:T(8,128)(2,1)}, bf16[2,4,4,40,3200]{4,3,2,1,0:T(8,128)(2,1)}, bf16[2,4,4,200,640]{4,3,2,1,0:T(8,128)(2,1)}, f32[10,2,320...) custom-call(bf16[2,4,4,40,1536]{4,3,2,1,0:T(8,128)(2,1)S(1)} %get-tu, ...), custom_call_target="tpu_custom_call" | custom-call | tf_op jit(solution)/shard_map/put/pallas_call | solution.py:472

commit v6 on v5

--- a/solution.py
+++ b/solution.py
@@ -459,7 +459,7 @@
 def put_kernel(*refs):
     n = len(HALVES)
     ins, outs, sem = refs[: 3 * n + 6], refs[3 * n + 6 : -1], refs[-1]
-    pairs = [(ins[w * n + h], outs[w].at[:, :, :, :, pl.ds(*COLS[w][h])]) for w in WEIGHTS for h in HALVES]
+    pairs = [(ins[w * n + h].at[l], outs[w].at[l, :, :, :, pl.ds(*COLS[w][h])]) for w in WEIGHTS for h in HALVES for l in LAYERS]
     pairs += zip(ins[3 * n :], outs[3:], strict=True)
     copies = [pltpu.make_async_copy(a, b, sem.at[i]) for i, (a, b) in enumerate(pairs)]
     for copy in copies:
@@ -474,7 +474,7 @@
         out_shape=[jax.ShapeDtypeStruct(s, BF16) for s in SHAPES] + [jax.ShapeDtypeStruct(s, F32) for s in MOMENTS * 2],
         in_specs=[ANYWHERE] * len(arrays),
         out_specs=[IN_HBM] * 9,
-        scratch_shapes=[pltpu.SemaphoreType.DMA((len(arrays),))],
+        scratch_shapes=[pltpu.SemaphoreType.DMA((2 * len(arrays),))],
         compiler_params=pltpu.CompilerParams(vmem_limit_bytes=2**20),
         name="put",
     )(*arrays)

time: 212 us -> 212 us (level)
  no operation moved by 1% of the time
where the time goes in v6:
time: 212 us
  Pallas kernels  212 us (100%)
    pallas_call x1, Pallas kernels, exchanged(): pl.pallas_call(kernel, out_shape=results + [vmem(s, F32) for s in MOMENTS...  203 us
    pallas_call x1, Pallas kernels, put(): pl.pallas_call(put_kernel, out_shape=[jax.ShapeDtypeStruct(s, BF16) for s...  8.87 us

profile of v6, /device:TPU:0, one launch (start us, length us, event | category | flops | bytes accessed | tf_op | source)
XLA Modules:
  0.0 212.2 jit_solution(6069955466868285306)
XLA Ops:
  0.6 202.7 %sum_step_gather.1 = (bf16[2,4,4,40,1536]{4,3,2,1,0:T(8,128)(2,1)S(1)}, bf16[2,4,4,40,1664]{4,3,2,1,0:T(8,128)(2,1)S(1)}, bf16[2,4,4,40,1536]{4,3,2,1,0:T(8,128)...) custom-call(bf16[2,4,4,40,3200]{4,3,2,1,0:T(8,128)(2,1)} %bitcast.21, ...), custom_call_target="tpu_custom_call" | custom-call | tf_op jit(solution)/shard_map/sum_step_gather/pallas_call | solution.py:425
  203.4 8.9 %put.1 = (bf16[2,4,4,40,3200]{4,3,2,1,0:T(8,128)(2,1)}, bf16[2,4,4,40,3200]{4,3,2,1,0:T(8,128)(2,1)}, bf16[2,4,4,200,640]{4,3,2,1,0:T(8,128)(2,1)}, f32[10,2,320...) custom-call(bf16[2,4,4,40,1536]{4,3,2,1,0:T(8,128)(2,1)S(1)} %get-tu, ...), custom_call_target="tpu_custom_call" | custom-call | tf_op jit(solution)/shard_map/put/pallas_call | solution.py:472
